TPU v7x, 32 devices: a whole 2x2x4 slice. The times are simulated.
32 devices in a mesh: dp: 2 (over x), tp: 4 (over z), pp: 4 (over y, core).
Axes of the slice: x: 2, y: 2, z: 4, core: 2. Of those that a mesh axis runs over, the one named last changes fastest.
Arguments:
- x_in: bfloat16 [4, 1, 1024, 768], P('dp'), parts along dimension 0
- g_out: float32 [4, 1, 1024, 768], P('dp'), parts along dimension 0
- ln1_gain: float32 [4, 768], P('pp')
- ln1_bias: float32 [4, 768], P('pp')
- w_qkv: bfloat16 [4, 768, 12, 3, 64], P('pp', None, 'tp')
- b_qkv: bfloat16 [4, 12, 3, 64], P('pp', 'tp')
- w_out: bfloat16 [4, 12, 64, 768], P('pp', 'tp')
- b_out: bfloat16 [4, 768], P('pp')
- ln2_gain: float32 [4, 768], P('pp')
- ln2_bias: float32 [4, 768], P('pp')
- w_up: bfloat16 [4, 768, 3072], P('pp', None, 'tp')
- b_up: bfloat16 [4, 3072], P('pp', 'tp')
- w_down: bfloat16 [4, 3072, 768], P('pp', 'tp')
- b_down: bfloat16 [4, 768], P('pp')
Outputs:
- output 1: bfloat16 [4, 1, 1024, 768], P('dp'), parts along dimension 0
- output 2: float32 [8, 768], P(('dp', 'pp')), parts along dimension 0
- output 3: float32 [8, 768], P(('dp', 'pp')), parts along dimension 0
- output 4: float32 [8, 768, 12, 3, 64], P(('dp', 'pp'), None, 'tp'), parts along dimension 0
- output 5: float32 [8, 12, 3, 64], P(('dp', 'pp'), 'tp'), parts along dimension 0
- output 6: float32 [8, 12, 64, 768], P(('dp', 'pp'), 'tp'), parts along dimension 0
- output 7: float32 [8, 768], P(('dp', 'pp')), parts along dimension 0
- output 8: float32 [8, 768], P(('dp', 'pp')), parts along dimension 0
- output 9: float32 [8, 768], P(('dp', 'pp')), parts along dimension 0
- output 10: float32 [8, 768, 3072], P(('dp', 'pp'), None, 'tp'), parts along dimension 0
- output 11: float32 [8, 3072], P(('dp', 'pp'), 'tp'), parts along dimension 0
- output 12: float32 [8, 3072, 768], P(('dp', 'pp'), 'tp'), parts along dimension 0
- output 13: float32 [8, 768], P(('dp', 'pp')), parts along dimension 0
There are 2 independent parts. A program takes and returns all parts, laid end to end along the dimension named above; an argument that names none is the same for every part.
All inputs are finite; a program needn't handle non-finite values.
Results may differ from a plain program's by a relative error of at most 0.0183967.
Values are sent between devices in bfloat16 or wider.
A program may use at most 1 GiB of HBM per device.

v0:
```python
import jax
import jax.numpy as jnp
from jax import lax
from jax.sharding import PartitionSpec as P

ROPE_BASE = 10000.0
LN_EPS = 1e-5
STAGE_SPECS = (P('pp', None), P('pp', None), P('pp', None, 'tp', None, None), P('pp', 'tp', None, None), P('pp', 'tp', None, None), P('pp', None), P('pp', None), P('pp', None), P('pp', None, 'tp'), P('pp', 'tp'), P('pp', 'tp', None), P('pp', None))
GRAD_SPECS = (P(('dp', 'pp'), None), P(('dp', 'pp'), None), P(('dp', 'pp'), None, 'tp', None, None), P(('dp', 'pp'), 'tp', None, None), P(('dp', 'pp'), 'tp', None, None), P(('dp', 'pp'), None), P(('dp', 'pp'), None), P(('dp', 'pp'), None), P(('dp', 'pp'), None, 'tp'), P(('dp', 'pp'), 'tp'), P(('dp', 'pp'), 'tp', None), P(('dp', 'pp'), None))


def norm_core(hidden, gain, shift):
    center = hidden - jnp.mean(hidden, axis=-1, keepdims=True)
    var_term = jnp.mean(center * center, axis=-1, keepdims=True)
    return center * lax.rsqrt(var_term + LN_EPS) * gain + shift


def rotary_tables(seq_len, head_dim):
    rot_dim = head_dim // 4
    half_rot = rot_dim // 2
    inv_freq = ROPE_BASE ** (-(jnp.arange(half_rot, dtype=jnp.float32) * 2.0) / rot_dim)
    angles = jnp.arange(seq_len, dtype=jnp.float32)[:, None] * inv_freq[None, :]
    angles = jnp.concatenate([angles, angles], axis=-1)
    return jnp.cos(angles)[None, :, None, :], jnp.sin(angles)[None, :, None, :]


def apply_rotary(values, cos_tab, sin_tab):
    rot_dim = cos_tab.shape[-1]
    half_rot = rot_dim // 2
    rot_part = values[..., :rot_dim]
    turned = jnp.concatenate([-rot_part[..., half_rot:], rot_part[..., :half_rot]], axis=-1)
    return jnp.concatenate([rot_part * cos_tab + turned * sin_tab, values[..., rot_dim:]], axis=-1)


def attention_core(qkv_proj, cos_tab, sin_tab):
    head_dim = qkv_proj.shape[-1]
    seq_len = qkv_proj.shape[1]
    query = apply_rotary(qkv_proj[:, :, :, 0].astype(jnp.float32), cos_tab, sin_tab).astype(jnp.bfloat16)
    key_rot = apply_rotary(qkv_proj[:, :, :, 1].astype(jnp.float32), cos_tab, sin_tab).astype(jnp.bfloat16)
    value_part = qkv_proj[:, :, :, 2]
    scores = jnp.einsum('bqhe,bkhe->bhqk', query, key_rot, preferred_element_type=jnp.float32) * (head_dim ** -0.5)
    positions = jnp.arange(seq_len)
    causal = positions[:, None] >= positions[None, :]
    scores = jnp.where(causal, scores, -1e30)
    probs = jax.nn.softmax(scores, axis=-1).astype(jnp.bfloat16)
    return jnp.einsum('bhqk,bkhe->bqhe', probs, value_part, preferred_element_type=jnp.float32).astype(jnp.bfloat16)


def stage_forward(hidden, layer_wts, cos_tab, sin_tab):
    ln1_gain, ln1_bias, w_qkv, b_qkv, w_out, b_out, ln2_gain, ln2_bias, w_up, b_up, w_down, b_down = layer_wts
    hidden_f = hidden.astype(jnp.float32)
    normed_a = norm_core(hidden_f, ln1_gain, ln1_bias).astype(jnp.bfloat16)
    normed_m = norm_core(hidden_f, ln2_gain, ln2_bias).astype(jnp.bfloat16)
    qkv_proj = jnp.einsum('btd,dhce->bthce', normed_a, w_qkv, preferred_element_type=jnp.float32)
    qkv_proj = (qkv_proj + b_qkv.astype(jnp.float32)).astype(jnp.bfloat16)
    context = attention_core(qkv_proj, cos_tab, sin_tab)
    attn_part = jnp.einsum('bthe,hed->btd', context, w_out, preferred_element_type=jnp.float32)
    pre_act = jnp.einsum('btd,df->btf', normed_m, w_up, preferred_element_type=jnp.float32) + b_up.astype(jnp.float32)
    hidden_mlp = jax.nn.gelu(pre_act, approximate=False).astype(jnp.bfloat16)
    mlp_part = jnp.einsum('btf,fd->btd', hidden_mlp, w_down, preferred_element_type=jnp.float32)
    attn_sum = lax.psum(attn_part.astype(jnp.bfloat16), 'tp')
    mlp_sum = lax.psum(mlp_part.astype(jnp.bfloat16), 'tp')
    total = hidden_f + attn_sum.astype(jnp.float32) + b_out.astype(jnp.float32) + mlp_sum.astype(jnp.float32) + b_down.astype(jnp.float32)
    return total.astype(jnp.bfloat16)


def stage_backward(hidden, grad_out, layer_wts, cos_tab, sin_tab):
    ln1_gain, ln1_bias, w_qkv, b_qkv, w_out, b_out, ln2_gain, ln2_bias, w_up, b_up, w_down, b_down = layer_wts
    hidden_f = hidden.astype(jnp.float32)
    normed_a32, pull_ln1 = jax.vjp(norm_core, hidden_f, ln1_gain, ln1_bias)
    normed_m32, pull_ln2 = jax.vjp(norm_core, hidden_f, ln2_gain, ln2_bias)
    normed_a = normed_a32.astype(jnp.bfloat16)
    normed_m = normed_m32.astype(jnp.bfloat16)
    qkv_proj = jnp.einsum('btd,dhce->bthce', normed_a, w_qkv, preferred_element_type=jnp.float32)
    qkv_proj = (qkv_proj + b_qkv.astype(jnp.float32)).astype(jnp.bfloat16)
    context, pull_attn = jax.vjp(lambda proj: attention_core(proj, cos_tab, sin_tab), qkv_proj)
    pre_act = jnp.einsum('btd,df->btf', normed_m, w_up, preferred_element_type=jnp.float32) + b_up.astype(jnp.float32)
    hidden_mlp, pull_gelu = jax.vjp(lambda act_in: jax.nn.gelu(act_in, approximate=False), pre_act)
    hidden_mlp_b = hidden_mlp.astype(jnp.bfloat16)
    grad_f = grad_out.astype(jnp.float32)
    grad_bias_out = jnp.sum(grad_f, axis=(0, 1))
    grad_w_out = jnp.einsum('bthe,btd->hed', context, grad_out, preferred_element_type=jnp.float32)
    grad_context = jnp.einsum('btd,hed->bthe', grad_out, w_out, preferred_element_type=jnp.float32).astype(jnp.bfloat16)
    (grad_qkv,) = pull_attn(grad_context)
    grad_b_qkv = jnp.sum(grad_qkv.astype(jnp.float32), axis=(0, 1))
    grad_w_qkv = jnp.einsum('btd,bthce->dhce', normed_a, grad_qkv, preferred_element_type=jnp.float32)
    grad_norm_a = jnp.einsum('bthce,dhce->btd', grad_qkv, w_qkv, preferred_element_type=jnp.float32)
    grad_w_down = jnp.einsum('btf,btd->fd', hidden_mlp_b, grad_out, preferred_element_type=jnp.float32)
    grad_mlp = jnp.einsum('btd,fd->btf', grad_out, w_down, preferred_element_type=jnp.float32)
    (grad_pre,) = pull_gelu(grad_mlp)
    grad_b_up = jnp.sum(grad_pre, axis=(0, 1))
    grad_pre_b = grad_pre.astype(jnp.bfloat16)
    grad_w_up = jnp.einsum('btd,btf->df', normed_m, grad_pre_b, preferred_element_type=jnp.float32)
    grad_norm_m = jnp.einsum('btf,df->btd', grad_pre_b, w_up, preferred_element_type=jnp.float32)
    grad_h1, grad_ln1_gain, grad_ln1_bias = pull_ln1(grad_norm_a)
    grad_h2, grad_ln2_gain, grad_ln2_bias = pull_ln2(grad_norm_m)
    grad_branch = lax.psum((grad_h1 + grad_h2).astype(jnp.bfloat16), 'tp')
    grad_in = (grad_f + grad_branch.astype(jnp.float32)).astype(jnp.bfloat16)
    layer_grads = (grad_ln1_gain, grad_ln1_bias, grad_w_qkv, grad_b_qkv, grad_w_out, grad_bias_out, grad_ln2_gain, grad_ln2_bias, grad_w_up, grad_b_up, grad_w_down, grad_bias_out)
    return grad_in, layer_grads


def solution(mesh):
    n_stages = mesh.shape['pp']
    tp_size = mesh.shape['tp']
    fwd_perm = [(src_stage, src_stage + 1) for src_stage in range(n_stages - 1)]
    bwd_perm = [(src_stage + 1, src_stage) for src_stage in range(n_stages - 1)]

    def device_fn(x_in, g_out, ln1_gain, ln1_bias, w_qkv, b_qkv, w_out, b_out, ln2_gain, ln2_bias, w_up, b_up, w_down, b_down):
        layer_wts = (ln1_gain[0], ln1_bias[0], w_qkv[0], b_qkv[0], w_out[0], b_out[0], ln2_gain[0], ln2_bias[0], w_up[0], b_up[0], w_down[0], b_down[0])
        stage_id = lax.axis_index('pp')
        tp_rank = lax.axis_index('tp')
        n_micro, n_rows, seq_len, width = x_in.shape
        cos_tab, sin_tab = rotary_tables(seq_len, w_qkv.shape[-1])
        piece_len = seq_len // tp_size
        n_steps = n_micro + n_stages - 1
        last_stage = n_stages - 1

        def pass_on(full, perm):
            own_rows = lax.dynamic_slice_in_dim(full, tp_rank * piece_len, piece_len, axis=1)
            arrived = lax.ppermute(own_rows, 'pp', perm)
            return lax.all_gather(arrived, 'tp', axis=1, tiled=True)

        def forward_body(step, carry):
            incoming, saved_in, y_all = carry
            micro_idx = step - stage_id
            valid = (micro_idx >= 0) & (micro_idx < n_micro)
            micro_slot = jnp.clip(micro_idx, 0, n_micro - 1)
            x_micro = lax.dynamic_index_in_dim(x_in, micro_slot, 0, keepdims=False)
            hidden = jnp.where(stage_id == 0, x_micro, incoming)
            result = stage_forward(hidden, layer_wts, cos_tab, sin_tab)
            old_in = lax.dynamic_index_in_dim(saved_in, micro_slot, 0, keepdims=False)
            saved_in = lax.dynamic_update_index_in_dim(saved_in, jnp.where(valid, hidden, old_in), micro_slot, 0)
            old_y = lax.dynamic_index_in_dim(y_all, micro_slot, 0, keepdims=False)
            keep_y = valid & (stage_id == last_stage)
            y_all = lax.dynamic_update_index_in_dim(y_all, jnp.where(keep_y, result, old_y), micro_slot, 0)
            return pass_on(result, fwd_perm), saved_in, y_all

        act_zero = jnp.zeros((n_rows, seq_len, width), jnp.bfloat16)
        fwd_state = lax.fori_loop(0, n_steps, forward_body, (act_zero, jnp.zeros_like(x_in), jnp.zeros_like(x_in)))
        saved_in = fwd_state[1]

        def backward_body(step, carry):
            incoming, grad_acc = carry
            micro_idx = step - (last_stage - stage_id)
            valid = (micro_idx >= 0) & (micro_idx < n_micro)
            micro_slot = jnp.clip(micro_idx, 0, n_micro - 1)
            hidden = lax.dynamic_index_in_dim(saved_in, micro_slot, 0, keepdims=False)
            g_micro = lax.dynamic_index_in_dim(g_out, micro_slot, 0, keepdims=False).astype(jnp.bfloat16)
            grad_out = jnp.where(stage_id == last_stage, g_micro, incoming)
            grad_in, layer_grads = stage_backward(hidden, grad_out, layer_wts, cos_tab, sin_tab)
            grad_acc = tuple(running + jnp.where(valid, update, 0.0) for running, update in zip(grad_acc, layer_grads))
            return pass_on(grad_in, bwd_perm), grad_acc

        grad_init = tuple(jnp.zeros(weight.shape, jnp.float32) for weight in layer_wts)
        bwd_state = lax.fori_loop(0, n_steps, backward_body, (act_zero, grad_init))
        grads = list(bwd_state[1])
        for norm_pos in (0, 1, 6, 7):
            grads[norm_pos] = lax.psum(grads[norm_pos], 'tp')
        y_out = lax.psum(fwd_state[2], 'pp')
        return tuple([y_out] + [grad[None] for grad in grads])

    return jax.shard_map(device_fn, mesh=mesh, in_specs=(P('dp'), P('dp')) + STAGE_SPECS, out_specs=(P('dp'),) + GRAD_SPECS, check_vma=False)
```

profile of v0, /device:TPU:0, one launch (start us, length us, event | category | flops | bytes accessed | tf_op | source)
XLA Modules:
  0.0 2247.5 jit_solution(6793023861414727423)
XLA Ops:
  24.3 1104.5 %while.59 = (s32[]{:T(128)}, bf16[1,1024,768]{2,1,0:T(8,128)(2,1)}, bf16[2,1,1024,768]{3,2,1,0:T(8,128)(2,1)}, bf16[2,1,1024,768]{3,2,1,0:T(8,128)(2,1)}, pred[]...) while((s32[]{:T(128)}, bf16[1,1024,768]{2,1,0:T(8,128)(2,1)}, ...), condition=%wide.region_7.8_spmd, body=%wide.region_0.7_spmd.sunk | while | flops 4530852864 | bytes 119792944 | solution.py:140
  43.9 10.8 fusion.323
  54.7 7.6 fusion.324
  62.3 11.7 fusion.318
  76.2 122.0 %all-reduce.21.cloned.1.call-done = (bf16[1,1024,768]{2,1,0:T(8,128)(2,1)}, bf16[1,1024,768]{2,1,0:T(8,128)(2,1)}) async-done(((bf16[1,1024,768]{2,1,0:T(8,128)(2,1)}, bf16[1,1024,768]{2,1,0:T(8,128)(2,1)}), (bf16[1,1024,768]{2,1,0:T(8,128)(2,1)}, bf16[1,1024,768]{2,1,0:T(8,128)(2,1)})) %all-reduce.21.cloned.1.call-update) | async-done | bytes 3145744 | tf_op jit(solution)/shard_map/while/body/eval_jaxpr/psum | solution.py:62
  205.8 42.4 %all-gather.3.cloned.1.call-done = bf16[1,1024,768]{2,1,0:T(8,128)(2,1)} async-done(((bf16[1,256,768]{2,1,0:T(8,128)(2,1)}), bf16[1,1024,768]{2,1,0:T(8,128)(2,1)}) %all-gather.3.cloned.1.call-update) | async-done | bytes 1572880 | tf_op jit(solution)/shard_map/while/body/eval_jaxpr/all_gather | solution.py:122
  267.8 10.8 fusion.323
  278.6 7.6 fusion.324
  286.2 11.7 fusion.318
  300.1 118.4 %all-reduce.21.cloned.1.call-done = (bf16[1,1024,768]{2,1,0:T(8,128)(2,1)}, bf16[1,1024,768]{2,1,0:T(8,128)(2,1)}) async-done(((bf16[1,1024,768]{2,1,0:T(8,128)(2,1)}, bf16[1,1024,768]{2,1,0:T(8,128)(2,1)}), (bf16[1,1024,768]{2,1,0:T(8,128)(2,1)}, bf16[1,1024,768]{2,1,0:T(8,128)(2,1)})) %all-reduce.21.cloned.1.call-update) | async-done | bytes 3145744 | tf_op jit(solution)/shard_map/while/body/eval_jaxpr/psum | solution.py:62
  426.1 42.4 %all-gather.3.cloned.1.call-done = bf16[1,1024,768]{2,1,0:T(8,128)(2,1)} async-done(((bf16[1,256,768]{2,1,0:T(8,128)(2,1)}), bf16[1,1024,768]{2,1,0:T(8,128)(2,1)}) %all-gather.3.cloned.1.call-update) | async-done | bytes 1572880 | tf_op jit(solution)/shard_map/while/body/eval_jaxpr/all_gather | solution.py:122
  488.0 10.8 fusion.323
  498.8 7.6 fusion.324
  506.4 11.7 fusion.318
  520.3 118.4 %all-reduce.21.cloned.1.call-done = (bf16[1,1024,768]{2,1,0:T(8,128)(2,1)}, bf16[1,1024,768]{2,1,0:T(8,128)(2,1)}) async-done(((bf16[1,1024,768]{2,1,0:T(8,128)(2,1)}, bf16[1,1024,768]{2,1,0:T(8,128)(2,1)}), (bf16[1,1024,768]{2,1,0:T(8,128)(2,1)}, bf16[1,1024,768]{2,1,0:T(8,128)(2,1)})) %all-reduce.21.cloned.1.call-update) | async-done | bytes 3145744 | tf_op jit(solution)/shard_map/while/body/eval_jaxpr/psum | solution.py:62
  646.2 42.5 %all-gather.3.cloned.1.call-done = bf16[1,1024,768]{2,1,0:T(8,128)(2,1)} async-done(((bf16[1,256,768]{2,1,0:T(8,128)(2,1)}), bf16[1,1024,768]{2,1,0:T(8,128)(2,1)}) %all-gather.3.cloned.1.call-update) | async-done | bytes 1572880 | tf_op jit(solution)/shard_map/while/body/eval_jaxpr/all_gather | solution.py:122
  708.2 10.8 fusion.323
  719.0 7.6 fusion.324
  726.6 11.7 fusion.318
  740.5 118.4 %all-reduce.21.cloned.1.call-done = (bf16[1,1024,768]{2,1,0:T(8,128)(2,1)}, bf16[1,1024,768]{2,1,0:T(8,128)(2,1)}) async-done(((bf16[1,1024,768]{2,1,0:T(8,128)(2,1)}, bf16[1,1024,768]{2,1,0:T(8,128)(2,1)}), (bf16[1,1024,768]{2,1,0:T(8,128)(2,1)}, bf16[1,1024,768]{2,1,0:T(8,128)(2,1)})) %all-reduce.21.cloned.1.call-update) | async-done | bytes 3145744 | tf_op jit(solution)/shard_map/while/body/eval_jaxpr/psum | solution.py:62
  866.4 42.4 %all-gather.3.cloned.1.call-done = bf16[1,1024,768]{2,1,0:T(8,128)(2,1)} async-done(((bf16[1,256,768]{2,1,0:T(8,128)(2,1)}), bf16[1,1024,768]{2,1,0:T(8,128)(2,1)}) %all-gather.3.cloned.1.call-update) | async-done | bytes 1572880 | tf_op jit(solution)/shard_map/while/body/eval_jaxpr/all_gather | solution.py:122
  928.3 10.8 fusion.323
  939.1 7.6 fusion.324
  946.7 11.7 fusion.318
  960.6 118.4 %all-reduce.21.cloned.1.call-done = (bf16[1,1024,768]{2,1,0:T(8,128)(2,1)}, bf16[1,1024,768]{2,1,0:T(8,128)(2,1)}) async-done(((bf16[1,1024,768]{2,1,0:T(8,128)(2,1)}, bf16[1,1024,768]{2,1,0:T(8,128)(2,1)}), (bf16[1,1024,768]{2,1,0:T(8,128)(2,1)}, bf16[1,1024,768]{2,1,0:T(8,128)(2,1)})) %all-reduce.21.cloned.1.call-update) | async-done | bytes 3145744 | tf_op jit(solution)/shard_map/while/body/eval_jaxpr/psum | solution.py:62
  1086.5 42.4 %all-gather.3.cloned.1.call-done = bf16[1,1024,768]{2,1,0:T(8,128)(2,1)} async-done(((bf16[1,256,768]{2,1,0:T(8,128)(2,1)}), bf16[1,1024,768]{2,1,0:T(8,128)(2,1)}) %all-gather.3.cloned.1.call-update) | async-done | bytes 1572880 | tf_op jit(solution)/shard_map/while/body/eval_jaxpr/all_gather | solution.py:122
  1130.2 1035.6 %while.60 = (s32[]{:T(128)}, bf16[1,1024,768]{2,1,0:T(8,128)(2,1)}, f32[768]{0:T(1024)}, f32[768]{0:T(1024)}, f32[768,3,3,64]{0,3,2,1:T(8,128)}, /*index=5*/f32[...) while((s32[]{:T(128)}, bf16[1,1024,768]{2,1,0:T(8,128)(2,1)}, ...), condition=%wide.region_27.28_spmd.clone, body=%wide.region_9.27_spmd.clone.sunk | while | flops 11997704192 | bytes 344378208 | solution.py:156
  1163.6 9.1 fusion.354
  1175.1 10.3 divide_convert_fusion.12
  1186.0 9.5 fusion.357
  1195.5 8.8 fusion.356
  1212.6 9.5 fusion.347
  1247.0 61.9 %all-reduce.23.cloned.1.call-done = bf16[1,1024,768]{2,1,0:T(8,128)(2,1)} async-done(((bf16[1,1024,768]{2,1,0:T(8,128)(2,1)}), bf16[1,1024,768]{2,1,0:T(8,128)(2,1)}) %all-reduce.23.cloned.1.call-update) | async-done | bytes 1572880 | tf_op jit(solution)/shard_map/while/body/eval_jaxpr/psum | solution.py:97
  1335.6 19.0 all-gather.5.cloned.1.call-done
  1366.3 9.1 fusion.354
  1377.9 10.3 divide_convert_fusion.12
  1388.8 9.5 fusion.357
  1398.3 8.8 fusion.356
  1415.4 9.5 fusion.347
  1453.1 58.5 %all-reduce.23.cloned.1.call-done = bf16[1,1024,768]{2,1,0:T(8,128)(2,1)} async-done(((bf16[1,1024,768]{2,1,0:T(8,128)(2,1)}), bf16[1,1024,768]{2,1,0:T(8,128)(2,1)}) %all-reduce.23.cloned.1.call-update) | async-done | bytes 1572880 | tf_op jit(solution)/shard_map/while/body/eval_jaxpr/psum | solution.py:97
  1539.5 17.9 all-gather.5.cloned.1.call-done
  1569.1 9.1 fusion.354
  1580.6 10.3 divide_convert_fusion.12
  1591.6 9.5 fusion.357
  1601.1 8.8 fusion.356
  1618.2 9.5 fusion.347
  1655.9 58.5 %all-reduce.23.cloned.1.call-done = bf16[1,1024,768]{2,1,0:T(8,128)(2,1)} async-done(((bf16[1,1024,768]{2,1,0:T(8,128)(2,1)}), bf16[1,1024,768]{2,1,0:T(8,128)(2,1)}) %all-reduce.23.cloned.1.call-update) | async-done | bytes 1572880 | tf_op jit(solution)/shard_map/while/body/eval_jaxpr/psum | solution.py:97
  1742.3 17.9 all-gather.5.cloned.1.call-done
  1771.9 9.1 fusion.354
  1783.4 10.3 divide_convert_fusion.12
  1794.4 9.5 fusion.357
  1803.8 8.8 fusion.356
  1820.9 9.5 fusion.347
  1858.7 58.4 %all-reduce.23.cloned.1.call-done = bf16[1,1024,768]{2,1,0:T(8,128)(2,1)} async-done(((bf16[1,1024,768]{2,1,0:T(8,128)(2,1)}), bf16[1,1024,768]{2,1,0:T(8,128)(2,1)}) %all-reduce.23.cloned.1.call-update) | async-done | bytes 1572880 | tf_op jit(solution)/shard_map/while/body/eval_jaxpr/psum | solution.py:97
  1945.6 17.4 all-gather.5.cloned.1.call-done
  1974.7 9.1 fusion.354
  1986.2 10.3 divide_convert_fusion.12
  1997.2 9.5 fusion.357
  2006.6 8.8 fusion.356
  2023.7 9.5 fusion.347
  2061.5 58.4 %all-reduce.23.cloned.1.call-done = bf16[1,1024,768]{2,1,0:T(8,128)(2,1)} async-done(((bf16[1,1024,768]{2,1,0:T(8,128)(2,1)}), bf16[1,1024,768]{2,1,0:T(8,128)(2,1)}) %all-reduce.23.cloned.1.call-update) | async-done | bytes 1572880 | tf_op jit(solution)/shard_map/while/body/eval_jaxpr/psum | solution.py:97
  2148.4 17.4 all-gather.5.cloned.1.call-done
  2168.9 17.4 all-reduce.12
  2186.3 49.7 %all-reduce.19.cloned.1.call-done = bf16[2,1,1024,768]{3,2,1,0:T(8,128)(2,1)} async-done(((bf16[2,1,1024,768]{3,2,1,0:T(8,128)(2,1)}), bf16[2,1,1024,768]{3,2,1,0:T(8,128)(2,1)}) %all-reduce.19.cloned.1.call-update) | async-done | bytes 3145744 | tf_op jit(solution)/shard_map/psum | solution.py:160
  (1138 shorter events, 559.0 us)
Async XLA Ops:
  24.3 173.9 %all-reduce.21.cloned.1.call-start = ((), (), s32[]{:S(2)}) async-start(), calls=%async_computation.1 | async-start | bytes 6291456 | tf_op jit(solution)/shard_map/while/body/eval_jaxpr/psum | solution.py:62
  43.9 10.8 copy-start.65
  74.0 174.2 %all-gather.3.cloned.1.call-start = ((), (), s32[]{:S(2)}) async-start(), calls=%async_computation.2 | async-start | bytes 1966080 | tf_op jit(solution)/shard_map/while/body/eval_jaxpr/all_gather | solution.py:122
  202.4 2.7 collective-permute-start
  248.2 170.2 %all-reduce.21.cloned.1.call-start = ((), (), s32[]{:S(2)}) async-start(), calls=%async_computation.1 | async-start | bytes 6291456 | tf_op jit(solution)/shard_map/while/body/eval_jaxpr/psum | solution.py:62
  267.8 10.8 copy-start.65
  297.9 170.5 %all-gather.3.cloned.1.call-start = ((), (), s32[]{:S(2)}) async-start(), calls=%async_computation.2 | async-start | bytes 1966080 | tf_op jit(solution)/shard_map/while/body/eval_jaxpr/all_gather | solution.py:122
  422.5 2.8 collective-permute-start
  468.4 170.2 %all-reduce.21.cloned.1.call-start = ((), (), s32[]{:S(2)}) async-start(), calls=%async_computation.1 | async-start | bytes 6291456 | tf_op jit(solution)/shard_map/while/body/eval_jaxpr/psum | solution.py:62
  488.0 10.8 copy-start.65
  518.1 170.5 %all-gather.3.cloned.1.call-start = ((), (), s32[]{:S(2)}) async-start(), calls=%async_computation.2 | async-start | bytes 1966080 | tf_op jit(solution)/shard_map/while/body/eval_jaxpr/all_gather | solution.py:122
  642.8 2.7 collective-permute-start
  688.7 170.2 %all-reduce.21.cloned.1.call-start = ((), (), s32[]{:S(2)}) async-start(), calls=%async_computation.1 | async-start | bytes 6291456 | tf_op jit(solution)/shard_map/while/body/eval_jaxpr/psum | solution.py:62
  708.2 10.8 copy-start.65
  738.3 170.4 %all-gather.3.cloned.1.call-start = ((), (), s32[]{:S(2)}) async-start(), calls=%async_computation.2 | async-start | bytes 1966080 | tf_op jit(solution)/shard_map/while/body/eval_jaxpr/all_gather | solution.py:122
  863.0 2.7 collective-permute-start
  908.8 170.2 %all-reduce.21.cloned.1.call-start = ((), (), s32[]{:S(2)}) async-start(), calls=%async_computation.1 | async-start | bytes 6291456 | tf_op jit(solution)/shard_map/while/body/eval_jaxpr/psum | solution.py:62
  928.3 10.8 copy-start.65
  958.5 170.4 %all-gather.3.cloned.1.call-start = ((), (), s32[]{:S(2)}) async-start(), calls=%async_computation.2 | async-start | bytes 1966080 | tf_op jit(solution)/shard_map/while/body/eval_jaxpr/all_gather | solution.py:122
  1083.1 2.7 collective-permute-start
  1151.9 157.0 %all-reduce.23.cloned.1.call-start = ((), (), s32[]{:S(2)}) async-start(), calls=%async_computation.3 | async-start | bytes 3145728 | tf_op jit(solution)/shard_map/while/body/eval_jaxpr/psum | solution.py:97
  1162.9 9.8 copy-start.21
  1175.1 10.4 copy-start.14
  1175.1 11.0 copy-start.28
  1212.6 9.6 copy-start.25
  1240.8 113.8 %all-gather.5.cloned.1.call-start = ((), (), s32[]{:S(2)}) async-start(), calls=%async_computation.4 | async-start | bytes 1966080 | tf_op jit(solution)/shard_map/while/body/eval_jaxpr/all_gather | solution.py:122
  1310.1 6.6 collective-permute-start.1
  1329.7 25.0 %copy-start.32 = (f32[1,768]{1,0:T(1,128)S(1)}, f32[1,768]{1,0:T(1,128)}, u32[]{:S(2)}) copy-start(f32[1,768]{1,0:T(1,128)} %copy-done.31) | copy-start | bytes 9220 | tf_op jit(solution)/shard_map/while
  1329.7 24.9 %copy-start.38 = (bf16[768]{0:T(1024)(128)(2,1)S(1)}, bf16[768]{0:T(1024)(128)(2,1)}, u32[]{:S(2)}) copy-start(bf16[768]{0:T(1024)(128)(2,1)} %copy-done.37) | copy-start | bytes 4612 | tf_op jit(solution)/shard_map/while
  1354.6 157.0 %all-reduce.23.cloned.1.call-start = ((), (), s32[]{:S(2)}) async-start(), calls=%async_computation.3 | async-start | bytes 3145728 | tf_op jit(solution)/shard_map/while/body/eval_jaxpr/psum | solution.py:97
  1365.7 9.8 copy-start.21
  1377.8 10.4 copy-start.14
  1377.8 11.0 copy-start.28
  1415.3 9.6 copy-start.25
  1443.5 113.9 %all-gather.5.cloned.1.call-start = ((), (), s32[]{:S(2)}) async-start(), calls=%async_computation.4 | async-start | bytes 1966080 | tf_op jit(solution)/shard_map/while/body/eval_jaxpr/all_gather | solution.py:122
  1512.9 6.6 collective-permute-start.1
  1532.9 24.5 %copy-start.32 = (f32[1,768]{1,0:T(1,128)S(1)}, f32[1,768]{1,0:T(1,128)}, u32[]{:S(2)}) copy-start(f32[1,768]{1,0:T(1,128)} %copy-done.31) | copy-start | bytes 9220 | tf_op jit(solution)/shard_map/while
  1532.9 24.5 %copy-start.38 = (bf16[768]{0:T(1024)(128)(2,1)S(1)}, bf16[768]{0:T(1024)(128)(2,1)}, u32[]{:S(2)}) copy-start(bf16[768]{0:T(1024)(128)(2,1)} %copy-done.37) | copy-start | bytes 4612 | tf_op jit(solution)/shard_map/while
  1557.4 157.0 %all-reduce.23.cloned.1.call-start = ((), (), s32[]{:S(2)}) async-start(), calls=%async_computation.3 | async-start | bytes 3145728 | tf_op jit(solution)/shard_map/while/body/eval_jaxpr/psum | solution.py:97
  1568.5 9.8 copy-start.21
  1580.6 10.4 copy-start.14
  1580.6 11.0 copy-start.28
  1618.1 9.6 copy-start.25
  1646.3 113.8 %all-gather.5.cloned.1.call-start = ((), (), s32[]{:S(2)}) async-start(), calls=%async_computation.4 | async-start | bytes 1966080 | tf_op jit(solution)/shard_map/while/body/eval_jaxpr/all_gather | solution.py:122
  1715.7 6.6 collective-permute-start.1
  1735.6 24.5 %copy-start.32 = (f32[1,768]{1,0:T(1,128)S(1)}, f32[1,768]{1,0:T(1,128)}, u32[]{:S(2)}) copy-start(f32[1,768]{1,0:T(1,128)} %copy-done.31) | copy-start | bytes 9220 | tf_op jit(solution)/shard_map/while
  1735.7 24.5 %copy-start.38 = (bf16[768]{0:T(1024)(128)(2,1)S(1)}, bf16[768]{0:T(1024)(128)(2,1)}, u32[]{:S(2)}) copy-start(bf16[768]{0:T(1024)(128)(2,1)} %copy-done.37) | copy-start | bytes 4612 | tf_op jit(solution)/shard_map/while
  1760.2 157.0 %all-reduce.23.cloned.1.call-start = ((), (), s32[]{:S(2)}) async-start(), calls=%async_computation.3 | async-start | bytes 3145728 | tf_op jit(solution)/shard_map/while/body/eval_jaxpr/psum | solution.py:97
  1771.3 9.8 copy-start.21
  1783.4 10.4 copy-start.14
  1783.4 11.0 copy-start.28
  1849.1 113.9 %all-gather.5.cloned.1.call-start = ((), (), s32[]{:S(2)}) async-start(), calls=%async_computation.4 | async-start | bytes 1966080 | tf_op jit(solution)/shard_map/while/body/eval_jaxpr/all_gather | solution.py:122
  1918.5 6.6 collective-permute-start.1
  1939.0 24.0 %copy-start.32 = (f32[1,768]{1,0:T(1,128)S(1)}, f32[1,768]{1,0:T(1,128)}, u32[]{:S(2)}) copy-start(f32[1,768]{1,0:T(1,128)} %copy-done.31) | copy-start | bytes 9220 | tf_op jit(solution)/shard_map/while
  1939.0 24.0 %copy-start.38 = (bf16[768]{0:T(1024)(128)(2,1)S(1)}, bf16[768]{0:T(1024)(128)(2,1)}, u32[]{:S(2)}) copy-start(bf16[768]{0:T(1024)(128)(2,1)} %copy-done.37) | copy-start | bytes 4612 | tf_op jit(solution)/shard_map/while
  1963.0 157.0 %all-reduce.23.cloned.1.call-start = ((), (), s32[]{:S(2)}) async-start(), calls=%async_computation.3 | async-start | bytes 3145728 | tf_op jit(solution)/shard_map/while/body/eval_jaxpr/psum | solution.py:97
  1974.1 9.8 copy-start.21
  1986.2 10.4 copy-start.14
  1986.2 11.0 copy-start.28
  2051.9 113.9 %all-gather.5.cloned.1.call-start = ((), (), s32[]{:S(2)}) async-start(), calls=%async_computation.4 | async-start | bytes 1966080 | tf_op jit(solution)/shard_map/while/body/eval_jaxpr/all_gather | solution.py:122
  2121.3 6.6 collective-permute-start.1
  2141.7 24.0 %copy-start.32 = (f32[1,768]{1,0:T(1,128)S(1)}, f32[1,768]{1,0:T(1,128)}, u32[]{:S(2)}) copy-start(f32[1,768]{1,0:T(1,128)} %copy-done.31) | copy-start | bytes 9220 | tf_op jit(solution)/shard_map/while
  2141.8 24.0 %copy-start.38 = (bf16[768]{0:T(1024)(128)(2,1)S(1)}, bf16[768]{0:T(1024)(128)(2,1)}, u32[]{:S(2)}) copy-start(bf16[768]{0:T(1024)(128)(2,1)} %copy-done.37) | copy-start | bytes 4612 | tf_op jit(solution)/shard_map/while
  2165.8 70.1 %all-reduce.19.cloned.1.call-start = ((), (), s32[]{:S(2)}) async-start(), calls=%async_computation | async-start | bytes 6291456 | tf_op jit(solution)/shard_map/psum | solution.py:160
  (291 other events, 1151.1 us)
Sparse Core Ops, SparseCore 0:
  74.2 124.0 all-reduce.20
  206.0 42.2 all-gather.2
  298.0 120.3 all-reduce.20
  426.2 42.2 all-gather.2
  518.2 120.3 all-reduce.20
  646.3 42.3 all-gather.2
  738.5 120.3 all-reduce.20
  866.5 42.2 all-gather.2
  958.6 120.3 all-reduce.20
  1086.6 42.2 all-gather.2
  1240.9 67.8 all-reduce.22
  1316.9 37.6 all-gather.4
  1443.7 67.9 all-reduce.22
  1519.7 37.6 all-gather.4
  1646.4 67.9 all-reduce.22
  1722.4 37.6 all-gather.4
  1849.2 67.9 all-reduce.22
  1925.2 37.6 all-gather.4
  2052.0 67.9 all-reduce.22
  2128.0 37.6 all-gather.4
Sparse Core Ops, SparseCore 1:
  2168.7 67.2 all-reduce.18
where the time goes:
time: 2270 us; the launch traced here: 2250 us
  waiting for transfers between devices  1250 us (55%)
  matrix products  583 us (26%)
  other arithmetic  266 us (12%)
  local copies, waits for them, and re-layouts  75 us (3%)
  loops' own time  26.3 us (1%)
    psum x5, waiting for transfers between devices, stage_forward(): mlp_sum = lax.psum(mlp_part.astype(jnp.bfloat16), 'tp')  595 us
    all_gather x10, waiting for transfers between devices, pass_on(): return lax.all_gather(arrived, 'tp', axis=1, tiled=True)  301 us
    psum x5, waiting for transfers between devices, stage_backward(): grad_branch = lax.psum((grad_h1 + grad_h2).astype(jnp.bfloat16), 'tp')  296 us
    sub x10, matrix products, attention_core(): probs = jax.nn.softmax(scores, axis=-1).astype(jnp.bfloat16)  99.5 us
    dot_general x10, matrix products, attention_core(): jnp.einsum('bqhe,bkhe->bhqk', query, key_rot, preferred_element_type=jnp....  91.2 us
    dot_general x10, matrix products, attention_core(): jnp.einsum('bhqk,bkhe->bqhe', probs, value_part, preferred_element_type=j...  75.8 us
    dot_general x5, matrix products, stage_forward(): jnp.einsum('btf,fd->btd', hidden_mlp, w_down, preferred_element_type=jnp....  58.5 us
    psum x1, waiting for transfers between devices, device_fn(): y_out = lax.psum(fwd_state[2], 'pp')  49.7 us
  transfers between devices with their start and end apart: 31, of which 26 were waited for; matrix products, arithmetic and copies ran while one was open for 8% of the time, Pallas kernels for 0%

commit v1 on v0

v1 whole, which is shorter than its diff:
```python
import functools

import jax
import jax.numpy as jnp
from jax import lax
from jax.experimental import pallas as pl
from jax.experimental.pallas import tpu as pltpu
from jax.sharding import PartitionSpec as P

BF = jnp.bfloat16
F32 = jnp.float32
ROPE_BASE = 10000.0
LN_EPS = 1e-5
HEADS = 3
HEAD = 64
PART = HEADS * HEAD
BLOCK = 256
ROWS = 2 * BLOCK
STAGE_SPECS = (P('pp', None), P('pp', None), P('pp', None, 'tp', None, None), P('pp', 'tp', None, None), P('pp', 'tp', None, None), P('pp', None), P('pp', None), P('pp', None), P('pp', None, 'tp'), P('pp', 'tp'), P('pp', 'tp', None), P('pp', None))
GRAD_SPECS = (P(('dp', 'pp'), None), P(('dp', 'pp'), None), P(('dp', 'pp'), None, 'tp', None, None), P(('dp', 'pp'), 'tp', None, None), P(('dp', 'pp'), 'tp', None, None), P(('dp', 'pp'), None), P(('dp', 'pp'), None), P(('dp', 'pp'), None), P(('dp', 'pp'), None, 'tp'), P(('dp', 'pp'), 'tp'), P(('dp', 'pp'), 'tp', None), P(('dp', 'pp'), None))
MESH_ID = pl.DeviceIdType.MESH


def dot(left, right, left_dim, right_dim):
    return lax.dot_general(left, right, (((left_dim,), (right_dim,)), ((), ())), preferred_element_type=F32)


def normalise(hidden):
    hidden_f = hidden.astype(F32)
    center = hidden_f - jnp.mean(hidden_f, axis=-1, keepdims=True)
    scale = lax.rsqrt(jnp.mean(center * center, axis=-1, keepdims=True) + LN_EPS)
    return center * scale, scale


def turn_matrix(width, transposed):
    row = lax.broadcasted_iota(jnp.int32, (width, width), 0)
    col = lax.broadcasted_iota(jnp.int32, (width, width), 1)
    if transposed:
        row, col = col, row
    dim = col % HEAD
    minus = (dim < 8) & (row == col + 8)
    plus = (dim >= 8) & (dim < 16) & (row == col - 8)
    return (plus.astype(F32) - minus.astype(F32)).astype(BF)


def rotate(values, cos_tab, sin_tab, transposed):
    turned = dot(values, turn_matrix(values.shape[1], transposed), 1, 0)
    return (values.astype(F32) * cos_tab + turned * sin_tab).astype(BF)


def causal_mask(core, block, n_keys):
    row = lax.broadcasted_iota(jnp.int32, (BLOCK, n_keys), 0)
    col = lax.broadcasted_iota(jnp.int32, (BLOCK, n_keys), 1)
    part = col // BLOCK
    starts = (core, 1 - core, 3 - core, 2 + core)
    start = jnp.where(part == 0, starts[0], jnp.where(part == 1, starts[1], jnp.where(part == 2, starts[2], starts[3])))
    mine = core if block == 0 else 3 - core
    return mine * BLOCK + row >= start * BLOCK + (col - part * BLOCK)


def interleave(own, other):
    return jnp.concatenate([own[:BLOCK], other[:BLOCK], own[BLOCK:], other[BLOCK:]], axis=0)


def pick(arr, head):
    return arr[:, head * HEAD:(head + 1) * HEAD]


def attend(query, keys, values, core):
    ctx_rows, lse_rows = [], []
    for block in range(2):
        n_keys = (2, 4)[block] * BLOCK
        mask = causal_mask(core, block, n_keys)
        ctxs, lses = [], []
        for head in range(HEADS):
            q_part = pick(query, head)[block * BLOCK:(block + 1) * BLOCK]
            scores = dot(q_part, pick(keys, head)[:n_keys], 1, 1) * (HEAD ** -0.5)
            scores = jnp.where(mask, scores, -1e30)
            top = jnp.max(scores, axis=-1, keepdims=True)
            expo = jnp.exp(scores - top)
            total = jnp.sum(expo, axis=-1, keepdims=True)
            probs = (expo / total).astype(BF)
            ctxs.append(dot(probs, pick(values, head)[:n_keys], 1, 0).astype(BF))
            lses.append(top + jnp.log(total))
        ctx_rows.append(jnp.concatenate(ctxs, axis=1))
        lse_rows.append(jnp.concatenate(lses, axis=1))
    return jnp.concatenate(ctx_rows, axis=0), jnp.concatenate(lse_rows, axis=0)


def attend_back(query, keys, values, lse, grad_ctx, core):
    dq_rows, dk_sum, dv_sum = [], None, None
    for block in range(2):
        n_keys = (2, 4)[block] * BLOCK
        mask = causal_mask(core, block, n_keys)
        rows = slice(block * BLOCK, (block + 1) * BLOCK)
        dqs, dks, dvs = [], [], []
        for head in range(HEADS):
            q_part = pick(query, head)[rows]
            k_part = pick(keys, head)[:n_keys]
            v_part = pick(values, head)[:n_keys]
            d_part = pick(grad_ctx, head)[rows]
            scores = dot(q_part, k_part, 1, 1) * (HEAD ** -0.5)
            probs = jnp.where(mask, jnp.exp(scores - lse[rows, head:head + 1]), 0.0)
            dprobs = dot(d_part, v_part, 1, 1).astype(BF).astype(F32)
            delta = jnp.sum(probs * dprobs, axis=-1, keepdims=True)
            dscores = (probs * (dprobs - delta) * (HEAD ** -0.5)).astype(BF)
            dqs.append(dot(dscores, k_part, 1, 0))
            dks.append(dot(dscores, q_part, 0, 0))
            dvs.append(dot(probs.astype(BF), d_part, 0, 0))
        dq_rows.append(jnp.concatenate(dqs, axis=1))
        dk_now, dv_now = jnp.concatenate(dks, axis=1), jnp.concatenate(dvs, axis=1)
        if block == 0:
            dk_sum, dv_sum = dk_now, dv_now
        else:
            dk_sum = jnp.concatenate([dk_now[:ROWS] + dk_sum, dk_now[ROWS:]], axis=0)
            dv_sum = jnp.concatenate([dv_now[:ROWS] + dv_sum, dv_now[ROWS:]], axis=0)
    return jnp.concatenate(dq_rows, axis=0), dk_sum, dv_sum


def sum_kernel(n_tp, part_ref, base_ref, shift_ref, out_ref, landed, send_a, recv_a, send_b, recv_b):
    rank = lax.axis_index('tp')
    share = out_ref.shape[0] // n_tp
    barrier = pltpu.get_barrier_semaphore()
    peers = [lax.rem(rank + step, n_tp) for step in range(1, n_tp)]
    for peer in peers:
        pl.semaphore_signal(barrier, inc=1, device_id={'tp': peer}, device_id_type=MESH_ID)
    pl.semaphore_wait(barrier, n_tp - 1)

    def rows_of(index):
        return pl.ds(pl.multiple_of(index * share, share), share)

    scatter = []
    for step, peer in enumerate(peers):
        copy = pltpu.make_async_remote_copy(
            src_ref=part_ref.at[rows_of(peer)], dst_ref=landed.at[step],
            send_sem=send_a.at[step], recv_sem=recv_a.at[step],
            device_id={'tp': peer}, device_id_type=MESH_ID)
        copy.start()
        scatter.append(copy)
    mine = rows_of(rank)
    total = base_ref[mine, :].astype(F32) + shift_ref[...] + part_ref[mine, :].astype(F32)
    for step, copy in enumerate(scatter):
        copy.wait_recv()
        total += landed[step].astype(F32)
    out_ref[mine, :] = total.astype(BF)
    gather = []
    for step, peer in enumerate(peers):
        copy = pltpu.make_async_remote_copy(
            src_ref=out_ref.at[mine], dst_ref=out_ref.at[mine],
            send_sem=send_b.at[step], recv_sem=recv_b.at[step],
            device_id={'tp': peer}, device_id_type=MESH_ID)
        copy.start()
        gather.append(copy)
    for copy in scatter:
        copy.wait_send()
    for copy in gather:
        copy.wait()


def sum_over_tp(part, base, shift, n_tp):
    rows, width = part.shape
    return pl.pallas_call(
        functools.partial(sum_kernel, n_tp),
        out_shape=jax.ShapeDtypeStruct((rows, width), BF),
        in_specs=[pl.BlockSpec(memory_space=pltpu.VMEM)] * 3,
        out_specs=pl.BlockSpec(memory_space=pltpu.VMEM),
        scratch_shapes=[pltpu.VMEM((n_tp - 1, rows // n_tp, width), BF)] + [pltpu.SemaphoreType.DMA((n_tp - 1,))] * 4,
        compiler_params=pltpu.CompilerParams(collective_id=0, has_side_effects=True),
        cost_estimate=pl.CostEstimate(flops=30_000_000_000, bytes_accessed=4_000_000, transcendentals=0),
    )(part, base, shift)


def solution(mesh):
    n_stages = mesh.shape['pp']
    n_tp = mesh.shape['tp']
    swap_core = [(stage, stage ^ 1) for stage in range(n_stages)]

    def device_fn(x_in, g_out, ln1_gain, ln1_bias, w_qkv, b_qkv, w_out, b_out, ln2_gain, ln2_bias, w_up, b_up, w_down, b_down):
        stage = lax.axis_index('pp')
        core = stage % 2
        seq_len, width = x_in.shape[2:]
        ffn = w_up.shape[2]

        def own_tokens(array):
            blocks = lax.dynamic_index_in_dim(array, stage // 2, 0, keepdims=False).reshape(4, BLOCK, width)
            first = lax.dynamic_index_in_dim(blocks, core, 0, keepdims=False)
            second = lax.dynamic_index_in_dim(blocks, 3 - core, 0, keepdims=False)
            return jnp.concatenate([first, second], axis=0).astype(BF)

        hidden = own_tokens(x_in)
        grad = own_tokens(g_out)

        half_rot = HEAD // 8
        inv_freq = ROPE_BASE ** (-(jnp.arange(half_rot, dtype=F32) * 2.0) / (2 * half_rot))
        spot = jnp.concatenate([core * BLOCK + jnp.arange(BLOCK), (3 - core) * BLOCK + jnp.arange(BLOCK)])
        angles = spot.astype(F32)[:, None] * inv_freq[None, :]
        still = jnp.zeros((ROWS, HEAD - 2 * half_rot), F32)
        cos_tab = jnp.tile(jnp.concatenate([jnp.cos(angles), jnp.cos(angles), still + 1.0], axis=1), (1, 2 * HEADS))
        sin_tab = jnp.tile(jnp.concatenate([jnp.sin(angles), jnp.sin(angles), still], axis=1), (1, 2 * HEADS))

        wq_rows = jnp.transpose(w_qkv[0], (2, 1, 3, 0)).reshape(3 * PART, width)
        bundle = jnp.concatenate([wq_rows, w_out[0].reshape(PART, width), w_up[0], w_down[0]], axis=0)
        bias_qkv = jnp.transpose(b_qkv[0], (1, 0, 2)).reshape(3 * PART).astype(F32)
        pad = jnp.zeros((width - 3 * PART,), F32)
        vectors = jnp.stack([ln1_gain[0], ln1_bias[0], ln2_gain[0], ln2_bias[0], b_out[0].astype(F32) + b_down[0].astype(F32), b_up[0].astype(F32), jnp.concatenate([bias_qkv, pad]), jnp.zeros((width,), F32)])

        first_wave = lax.ppermute(bundle, 'pp', [(0, 2), (2, 0)])
        held, first_wave = lax.optimization_barrier((bundle, first_wave))
        second_wave = lax.ppermute(held, 'pp', [(1, 3), (3, 1)])
        partner = lax.ppermute(bundle, 'pp', swap_core)
        first_pass = lax.ppermute(first_wave, 'pp', [(2, 3), (0, 1)])
        second_pass = lax.ppermute(second_wave, 'pp', [(3, 2), (1, 0)])
        all_vectors = lax.all_gather(vectors, 'pp')
        sources = (
            (bundle, partner, first_wave, first_pass),
            (partner, bundle, second_pass, second_wave),
            (first_wave, first_pass, bundle, partner),
            (second_pass, second_wave, partner, bundle),
        )

        def choose(options):
            return jnp.where(stage == 0, options[0], jnp.where(stage == 1, options[1], jnp.where(stage == 2, options[2], options[3])))

        cut = (3 * PART, 4 * PART, 4 * PART + width)
        saved = []
        for layer in range(n_stages):
            weights = choose(sources[layer])
            wq, wo, wu, wd = weights[:cut[0]], weights[cut[0]:cut[1]], weights[cut[1]:cut[2]], weights[cut[2]:]
            vec = all_vectors[layer]
            xhat, scale = normalise(hidden)
            normed_a = (xhat * vec[0] + vec[1]).astype(BF)
            normed_m = (xhat * vec[2] + vec[3]).astype(BF)
            qkv = (dot(normed_a, wq, 1, 1) + vec[6, :3 * PART]).astype(BF)
            turned = rotate(qkv[:, :2 * PART], cos_tab, sin_tab, False)
            query = turned[:, :PART]
            key_value = jnp.concatenate([turned[:, PART:], qkv[:, 2 * PART:]], axis=1)
            other = lax.ppermute(key_value, 'pp', swap_core)
            kv_all = interleave(key_value, other)
            context, lse = attend(query, kv_all[:, :PART], kv_all[:, PART:], core)
            pre_act = dot(normed_m, wu, 1, 0) + vec[5]
            active = jax.nn.gelu(pre_act, approximate=False).astype(BF)
            part = (dot(context, wo, 1, 0) + dot(active, wd, 1, 0)).astype(BF)
            saved.append((hidden, query, kv_all, context, lse, pre_act, weights))
            hidden = sum_over_tp(part, hidden, vec[4:5], n_tp)

        gathered = lax.all_gather(hidden, 'pp').reshape(2, 2, 2, BLOCK, width)
        y_out = jnp.stack([gathered[:, 0, 0], gathered[:, 1, 0], gathered[:, 1, 1], gathered[:, 0, 1]], axis=1).reshape(x_in.shape)

        big_grad = jnp.zeros(bundle.shape, F32)
        small = []
        zero_row = jnp.zeros((1, width), F32)
        for layer in reversed(range(n_stages)):
            hidden, query, kv_all, context, lse, pre_act, weights = saved[layer]
            wq, wo, wu, wd = weights[:cut[0]], weights[cut[0]:cut[1]], weights[cut[1]:cut[2]], weights[cut[2]:]
            vec = all_vectors[layer]
            xhat, scale = normalise(hidden)
            normed_a = (xhat * vec[0] + vec[1]).astype(BF)
            normed_m = (xhat * vec[2] + vec[3]).astype(BF)
            gauss = 0.5 * (1.0 + lax.erf(pre_act * (2.0 ** -0.5)))
            active = (pre_act * gauss).astype(BF)
            slope = gauss + pre_act * jnp.exp(-0.5 * pre_act * pre_act) * 0.3989422804014327
            grad_pre = dot(grad, wd, 1, 1) * slope
            grad_pre_b = grad_pre.astype(BF)
            grad_m = dot(grad_pre_b, wu, 1, 1)
            grad_ctx = dot(grad, wo, 1, 1).astype(BF)
            dq, dk_all, dv_all = attend_back(query, kv_all[:, :PART], kv_all[:, PART:], lse, grad_ctx, core)
            dkv = jnp.concatenate([dk_all, dv_all], axis=1).reshape(4, BLOCK, 2 * PART)
            back = lax.ppermute(jnp.concatenate([dkv[1], dkv[3]], axis=0), 'pp', swap_core)
            dkv = (jnp.concatenate([dkv[0], dkv[2]], axis=0) + back).astype(BF)
            dqk = rotate(jnp.concatenate([dq.astype(BF), dkv[:, :PART]], axis=1), cos_tab, sin_tab, True)
            grad_qkv = jnp.concatenate([dqk, dkv[:, PART:]], axis=1)
            grad_a = dot(grad_qkv, wq, 1, 0)
            small.append(jnp.stack([
                jnp.sum(grad_a * xhat, axis=0), jnp.sum(grad_a, axis=0), jnp.sum(grad_m * xhat, axis=0), jnp.sum(grad_m, axis=0),
                jnp.sum(grad.astype(F32), axis=0), jnp.sum(grad_pre, axis=0),
                jnp.concatenate([jnp.sum(grad_qkv.astype(F32), axis=0), pad]), pad_row(width)]))
            grad_big = jnp.concatenate([dot(grad_qkv, normed_a, 0, 0), dot(context, grad, 0, 0), dot(normed_m, grad_pre_b, 0, 0), dot(active, grad, 0, 0)], axis=0)
            if layer:
                grad_x = grad_a * vec[0] + grad_m * vec[2]
                branch = scale * (grad_x - jnp.mean(grad_x, axis=-1, keepdims=True) - xhat * jnp.mean(grad_x * xhat, axis=-1, keepdims=True))
                grad = sum_over_tp(branch.astype(BF), grad, zero_row, n_tp)
            near = lax.ppermute(grad_big.astype(BF), 'pp', [(layer ^ 1, layer), (layer ^ 3, layer ^ 2)])
            grad_big = grad_big + near.astype(F32)
            far = lax.ppermute(grad_big.astype(BF), 'pp', [(layer ^ 2, layer)])
            big_grad = jnp.where(stage == layer, grad_big + far.astype(F32), big_grad)

        small = lax.psum(jnp.stack(small[::-1]), 'pp')
        small = lax.dynamic_index_in_dim(small, stage, 0, keepdims=False)
        norms = lax.psum(small[:4], 'tp')
        grad_qkv = jnp.transpose(big_grad[:cut[0]].reshape(3, HEADS, HEAD, width), (3, 1, 0, 2))
        grads = (
            norms[0], norms[1], grad_qkv, jnp.transpose(small[6, :3 * PART].reshape(3, HEADS, HEAD), (1, 0, 2)),
            big_grad[cut[0]:cut[1]].reshape(HEADS, HEAD, width), small[4], norms[2], norms[3],
            big_grad[cut[1]:cut[2]], small[5], big_grad[cut[2]:], small[4])
        return tuple([y_out] + [item[None] for item in grads])

    return jax.shard_map(device_fn, mesh=mesh, in_specs=(P('dp'), P('dp')) + STAGE_SPECS, out_specs=(P('dp'),) + GRAD_SPECS, check_vma=False)


def pad_row(width):
    return jnp.zeros((width,), F32)
```

time: 2270 us -> 790 us (0.35)
  waiting for transfers between devices: 1250 us -> 79.8 us
  matrix products: 583 us -> 147 us
  Pallas kernels: 0 us -> 262 us
  other arithmetic: 266 us -> 112 us
  starting transfers between devices: 14 us -> 64.2 us
  loops' own time: 26.3 us -> 0 us
    psum x11 -> x1, waiting for transfers between devices: 941 us -> 0.02 us  [device_fn(): small = lax.psum(jnp.stack(small[::-1]), 'pp')]
    all_gather x10 -> x1, waiting for transfers between devices: 301 us -> 0.01 us  [device_fn(): gathered = lax.all_gather(hidden, 'pp').reshape(2, 2, 2, BLOCK, width)]
    dot_general x70 -> x200, matrix products: 437 us -> 147 us  [dot(): lax.dot_general(left, right, (((left_dim,), (right_dim,)), ((), ())), pre...]
    pallas_call x0 -> x7, Pallas kernels: none -> 262 us  [sum_over_tp(): pl.pallas_call(functools.partial(sum_kernel, n_tp), out_shape=jax.ShapeDt...]
    sub x10 -> x0, matrix products: 99.5 us -> none  [attention_core(): probs = jax.nn.softmax(scores, axis=-1).astype(jnp.bfloat16)]
    ppermute x10 -> x21, waiting for transfers between devices: 6.55 us -> 79.8 us  [the longest x4 45.2 us: device_fn(): far = lax.ppermute(grad_big.astype(BF), 'pp', [(layer ^ 2, layer)])]
    ppermute x10 -> x21, starting transfers between devices: 13.3 us -> 64.1 us  [the longest x4 27 us: device_fn(): other = lax.ppermute(key_value, 'pp', swap_core)]
    while x15 -> x0, matrix products: 45.9 us -> none
  transfers between devices with their start and end apart: 31 -> 23, of which waited for: 26 -> 3; matrix products, arithmetic and copies ran while one was open for 8% -> 23% of each run, Pallas kernels for 0% -> 18%
where the time goes in v1:
time: 790 us; the launch traced here: 780 us
  Pallas kernels  262 us (33%)
  matrix products  147 us (19%)
  other arithmetic  112 us (14%)
  waiting for transfers between devices  79.8 us (10%)
  starting transfers between devices  64.2 us (8%)
  local copies, waits for them, and re-layouts  62.4 us (8%)
  blocking collectives  31 us (4%)
  between operations  21 us (3%)
    pallas_call x7, Pallas kernels, sum_over_tp(): pl.pallas_call(functools.partial(sum_kernel, n_tp), out_shape=jax.ShapeDt...  262 us
    dot_general x200, matrix products, dot(): lax.dot_general(left, right, (((left_dim,), (right_dim,)), ((), ())), pre...  147 us
    ppermute x4, waiting for transfers between devices, device_fn(): far = lax.ppermute(grad_big.astype(BF), 'pp', [(layer ^ 2, layer)])  45.2 us
    ppermute x1, waiting for transfers between devices, device_fn(): first_wave = lax.ppermute(bundle, 'pp', [(0, 2), (2, 0)])  34.5 us
    ppermute x4, starting transfers between devices, device_fn(): other = lax.ppermute(key_value, 'pp', swap_core)  27 us
    psum x1, blocking collectives, device_fn(): norms = lax.psum(small[:4], 'tp')  25.5 us
    unnamed x838, local copies, waits for them, and re-layouts  22.3 us
    convert_element_type x4, other arithmetic, device_fn(): far = lax.ppermute(grad_big.astype(BF), 'pp', [(layer ^ 2, layer)])  17.7 us
  transfers between devices with their start and end apart: 23, of which 3 were waited for; matrix products, arithmetic and copies ran while one was open for 23% of the time, Pallas kernels for 18%

profile of v1, /device:TPU:0, one launch (start us, length us, event | category | flops | bytes accessed | tf_op | source)
XLA Modules:
  0.0 779.7 jit_solution(8505341910644467763)
XLA Ops:
  8.8 3.2 pad_maximum_fusion.4
  12.0 4.9 collective-permute-start.1
  17.1 3.8 constant_dynamic-slice_fusion
  21.9 34.5 %collective-permute-done.1 = bf16[2304,768]{1,0:T(8,128)(2,1)} collective-permute-done((bf16[2304,768]{1,0:T(8,128)(2,1)}, bf16[2304,768]{1,0:T(8,128)(2,1)}, u32[]{:S(2)}, u32[]{:S(2)}) %collective-permute-start.1) | collective-permute-done | bytes 3538976 | tf_op jit(solution)/shard_map/ppermute | solution.py:207
  56.4 3.1 collective-permute-start.2
  62.0 5.5 all-gather
  70.4 2.1 pad_maximum_fusion.6.base_ref
  74.0 2.5 collective-permute-start.4
  78.3 5.9 select_select_fusion.4
  85.8 1.5 collective-permute-start.3
  88.3 4.0 fusion.240
  102.0 23.1 %shard_map.237.base_ref = bf16[512,768]{1,0:T(8,128)(2,1)} custom-call(bf16[512,768]{1,0:T(8,128)(2,1)} %add_convert_fusion.3.part_ref, bf16[512,768]{1,0:T(8,128)(2,1)} %pad_maximum_fusion.6.base_ref, f32[1,768]{1,0:T(1,128)} %get-tuple-element.230.shift_ref), custom_call_target="tpu_custom_call" | custom-call | flops 30000001024 | bytes 4000000 | tf_op jit(solution)/shard_map/pallas_call | solution.py:162
  131.8 5.5 select_select_fusion.3
  139.8 25.2 %collective-permute-start.6 = (bf16[512,384]{0,1:T(8,128)(2,1)S(1)}, bf16[512,384]{0,1:T(8,128)(2,1)S(1)}, u32[]{:S(2)}, u32[]{:S(2)}) collective-permute-start(bf16[512,384]{0,1:T(8,128)(2,1)S(1)} %pad_maximum_fusion.29), channel_id=1, source_target_pairs={{0,1},{1,0},{2,3},{3,2},{4,5},{5,4},{6,7},{7,6},{8,9},{9,8},{10,11... | collective-permute-start | bytes 1179656 | tf_op jit(solution)/shard_map/ppermute | solution.py:237
  166.0 4.0 fusion.234
  181.7 37.8 %shard_map.238.base_ref = bf16[512,768]{1,0:T(8,128)(2,1)} custom-call(bf16[512,768]{1,0:T(8,128)(2,1)} %add_convert_fusion.2.part_ref, bf16[512,768]{1,0:T(8,128)(2,1)} %shard_map.237.base_ref, f32[1,768]{1,0:T(1,128)} %get-tuple-element.229.shift_ref), custom_call_target="tpu_custom_call" | custom-call | flops 30000001024 | bytes 4000000 | tf_op jit(solution)/shard_map/pallas_call | solution.py:162
  221.0 1.7 fusion.55
  222.7 2.0 fusion.136
  227.8 4.0 fusion.228
  244.1 41.3 %shard_map.239.base_ref = bf16[512,768]{1,0:T(8,128)(2,1)} custom-call(bf16[512,768]{1,0:T(8,128)(2,1)} %add_convert_fusion.1.part_ref, bf16[512,768]{1,0:T(8,128)(2,1)} %shard_map.238.base_ref, f32[1,768]{1,0:T(1,128)} %get-tuple-element.228.shift_ref), custom_call_target="tpu_custom_call" | custom-call | flops 30000001024 | bytes 4000000 | tf_op jit(solution)/shard_map/pallas_call | solution.py:162
  286.9 1.7 fusion.44
  288.7 2.2 fusion.137
  294.6 4.0 fusion.222
  299.8 2.4 fusion.465
  324.6 2.0 fusion.1010
  328.0 39.3 %shard_map.241.base_ref = bf16[512,768]{1,0:T(8,128)(2,1)} custom-call(bf16[512,768]{1,0:T(8,128)(2,1)} %fusion.41.part_ref, bf16[512,768]{1,0:T(8,128)(2,1)} %pad_maximum_fusion.11.base_ref, f32[1,768]{1,0:T(1,128)} %copy-done.213), custom_call_target="tpu_custom_call" | custom-call | flops 30000001024 | bytes 4000000 | tf_op jit(solution)/shard_map/pallas_call | solution.py:162
  367.4 1.5 convert_reduce_fusion.5
  368.9 1.6 convolution_convert_fusion.26
  386.2 3.4 fusion.1027
  398.5 2.1 fusion.154
  400.6 4.5 collective-permute-start.19
  406.1 3.9 fusion.462
  415.8 1.9 fusion.1007
  419.1 39.3 %shard_map.242.base_ref = bf16[512,768]{1,0:T(8,128)(2,1)} custom-call(bf16[512,768]{1,0:T(8,128)(2,1)} %fusion.52.part_ref, bf16[512,768]{1,0:T(8,128)(2,1)} %shard_map.241.base_ref, f32[1,768]{1,0:T(1,128)} %copy-done.213), custom_call_target="tpu_custom_call" | custom-call | flops 30000001024 | bytes 4000000 | tf_op jit(solution)/shard_map/pallas_call | solution.py:162
  459.9 1.6 convolution_convert_fusion.25
  475.8 3.4 fusion.1028
  484.6 2.1 fusion.155
  488.9 3.9 fusion.459
  492.8 2.3 fusion.258
  499.9 2.0 fusion.1004
  503.2 40.3 %shard_map.243 = bf16[512,768]{1,0:T(8,128)(2,1)} custom-call(bf16[512,768]{1,0:T(8,128)(2,1)} %fusion.63.part_ref, bf16[512,768]{1,0:T(8,128)(2,1)} %shard_map.242.base_ref, f32[1,768]{1,0:T(1,128)} %copy-done.213), custom_call_target="tpu_custom_call" | custom-call | flops 30000001024 | bytes 4000000 | tf_op jit(solution)/shard_map/pallas_call | solution.py:162
  544.9 1.6 convolution_convert_fusion.24
  560.7 3.5 fusion.1029
  573.0 2.0 fusion.156
  575.0 4.4 collective-permute-start.15
  582.0 3.8 fusion.456
  585.9 2.3 fusion.257
  594.9 2.0 fusion.524
  597.4 3.2 fusion.157
  601.9 40.7 %shard_map.240 = bf16[512,768]{1,0:T(8,128)(2,1)} custom-call(bf16[512,768]{1,0:T(8,128)(2,1)} %add_convert_fusion.part_ref, bf16[512,768]{1,0:T(8,128)(2,1)} %shard_map.239.base_ref, f32[1,768]{1,0:T(1,128)} %get-tuple-element.227.shift_ref), custom_call_target="tpu_custom_call" | custom-call | flops 30000001024 | bytes 4000000 | tf_op jit(solution)/shard_map/pallas_call | solution.py:162
  642.7 6.0 fusion.3
  648.7 2.6 collective-permute-start.20
  651.3 3.9 fusion.2
  655.3 5.5 collective-permute-start.18
  660.9 3.9 fusion.1
  664.8 2.5 collective-permute-start.16
  667.3 3.8 fusion
  676.6 25.5 %psum.15 = f32[4,768]{1,0:T(4,128)S(1)} all-reduce(f32[4,768]{1,0:T(4,128)} %dynamic-slice_bitcast_fusion.3), channel_id=1, replica_groups=mesh['dp'=2,'tp'=4,'pp'=4] {'tp'}, use_global_device_ids=true, to_apply=%region_115.116 | all-reduce | flops 3072 | bytes 24576 | tf_op jit(solution)/shard_map/psum | solution.py:289
  702.8 2.1 slice_bitcast_fusion.5
  705.4 1.9 copy.38
  707.3 38.7 %collective-permute-done.18 = bf16[2304,768]{1,0:T(8,128)(2,1)} collective-permute-done((bf16[2304,768]{1,0:T(8,128)(2,1)}, bf16[2304,768]{1,0:T(8,128)(2,1)}, u32[]{:S(2)}, u32[]{:S(2)}) %collective-permute-start.18) | collective-permute-done | bytes 3538976 | tf_op jit(solution)/shard_map/ppermute | solution.py:284
  746.0 6.5 collective-permute-done.14
  752.6 14.5 %select_select_fusion = f32[2304,768]{1,0:T(8,128)S(1)} fusion(bf16[2304,768]{1,0:T(8,128)(2,1)} %collective-permute-done.20, bf16[2304,768]{1,0:T(8,128)(2,1)} %collective-permute-done.18, bf16[2304,768]{1,0:T(8,128)(2,1)} %collective-permute-done.16, bf16[2304,768]{1,0:T(8,128)(2,1)} %collective-permute-done.14, ...), kind=kLoop, calls=%fused_computation.4 | loop fusion | flops 56623104 | bytes 63700996 | tf_op jit(solution)/shard_map/jit(_where)/select_n | solution.py:285
  768.0 2.5 slice_bitcast_fusion
  (1278 shorter events, 194.0 us)
Async XLA Ops:
  7.2 665.2 %all-reduce.7.cloned.1.call-start = ((), (), s32[]{:S(2)}) async-start(), calls=%async_computation | async-start | bytes 196608 | tf_op jit(solution)/shard_map/psum | solution.py:287
  12.0 44.4 %collective-permute-start.1 = (bf16[2304,768]{1,0:T(8,128)(2,1)}, bf16[2304,768]{1,0:T(8,128)(2,1)}, u32[]{:S(2)}, u32[]{:S(2)}) collective-permute-start(bf16[2304,768]{1,0:T(8,128)(2,1)} %pad_maximum_fusion.4), channel_id=1, source_target_pairs={{0,2},{2,0},{4,6},{6,4},{8,10},{10,8},{12,14},{14,12},{16,18},{18,... | collective-permute-start | bytes 10616840 | tf_op jit(solution)/shard_map/ppermute | solution.py:207
  16.9 61.3 %collective-permute-start = (bf16[2304,768]{1,0:T(8,128)(2,1)}, bf16[2304,768]{1,0:T(8,128)(2,1)S(1)}, u32[]{:S(2)}, u32[]{:S(2)}) collective-permute-start(bf16[2304,768]{1,0:T(8,128)(2,1)} %pad_maximum_fusion.4), channel_id=1, source_target_pairs={{0,1},{1,0},{2,3},{3,2},{4,5},{5,4},{6,7},{7,6},{8,9},{9,8},{10,11... | collective-permute-start | bytes 10616840 | tf_op jit(solution)/shard_map/ppermute | solution.py:210
  20.9 39.7 %copy-start.399 = (f32[1,768]{1,0:T(1,128)S(1)}, f32[1,768]{1,0:T(1,128)}, u32[]{:S(2)}) copy-start(f32[1,768]{1,0:T(1,128)} %param.16) | copy-start | bytes 9220
  56.4 21.9 %collective-permute-start.2 = (bf16[2304,768]{1,0:T(8,128)(2,1)}, bf16[2304,768]{1,0:T(8,128)(2,1)}, u32[]{:S(2)}, u32[]{:S(2)}) collective-permute-start(bf16[2304,768]{1,0:T(8,128)(2,1)} %collective-permute-done.1), channel_id=1, source_target_pairs={{2,3},{0,1},{6,7},{4,5},{10,11},{8,9},{14,15},{12,13},{18,19},{16,... | collective-permute-start | bytes 10616840 | tf_op jit(solution)/shard_map/ppermute | solution.py:211
  68.8 31.3 %copy-start.227 = (pred[512]{0:T(512)(128)(4,1)}, pred[512]{0:T(512)(128)(4,1)S(1)}, u32[]{:S(2)}) copy-start(pred[512]{0:T(512)(128)(4,1)S(1)} %fusion.724) | copy-start | bytes 1540
  68.9 16.4 %copy-start.234 = (pred[384]{0:T(512)(128)(4,1)}, pred[384]{0:T(512)(128)(4,1)S(1)}, u32[]{:S(2)}) copy-start(pred[384]{0:T(512)(128)(4,1)S(1)} %fusion.725) | copy-start | bytes 1156
  68.9 30.7 %copy-start.217 = (pred[1024]{0:T(1024)(128)(4,1)}, pred[1024]{0:T(1024)(128)(4,1)S(1)}, u32[]{:S(2)}) copy-start(pred[1024]{0:T(1024)(128)(4,1)S(1)} %fusion.718) | copy-start | bytes 3076
  68.9 16.3 %copy-start.182 = (s32[384]{0:T(512)}, s32[384]{0:T(512)S(1)}, u32[]{:S(2)}) copy-start(s32[384]{0:T(512)S(1)} %fusion.719) | copy-start | bytes 4612
  68.9 16.3 %copy-start.188 = (s32[384]{0:T(512)}, s32[384]{0:T(512)S(1)}, u32[]{:S(2)}) copy-start(s32[384]{0:T(512)S(1)} %iota_and_fusion.1) | copy-start | bytes 4612
  69.0 30.6 %copy-start.206 = (s32[256]{0:T(256)}, s32[256]{0:T(256)S(1)}, u32[]{:S(2)}) copy-start(s32[256]{0:T(256)S(1)} %get-tuple-element.299) | copy-start | bytes 3076
  69.0 31.1 %copy-start.175 = (s32[256]{0:T(256)}, s32[256]{0:T(256)S(1)}, u32[]{:S(2)}) copy-start(s32[256]{0:T(256)S(1)} %get-tuple-element.300) | copy-start | bytes 3076
  69.0 16.2 %copy-start.194 = (s32[384]{0:T(512)}, s32[384]{0:T(512)S(1)}, u32[]{:S(2)}) copy-start(s32[384]{0:T(512)S(1)} %get-tuple-element.301) | copy-start | bytes 4612
  69.1 16.2 %copy-start.200 = (s32[384]{0:T(512)}, s32[384]{0:T(512)S(1)}, u32[]{:S(2)}) copy-start(s32[384]{0:T(512)S(1)} %get-tuple-element.302) | copy-start | bytes 4612
  70.4 13.8 %copy-start.340 = (f32[768]{0:T(1024)}, f32[768]{0:T(1024)S(1)}, u32[]{:S(2)}) copy-start(f32[768]{0:T(1024)S(1)} %get-tuple-element.70) | copy-start | bytes 9220
  70.4 16.9 %copy-start.342 = (f32[768]{0:T(1024)}, f32[768]{0:T(1024)S(1)}, u32[]{:S(2)}) copy-start(f32[768]{0:T(1024)S(1)} %get-tuple-element.68) | copy-start | bytes 9220
  70.4 16.9 %copy-start.343 = (f32[768]{0:T(1024)}, f32[768]{0:T(1024)S(1)}, u32[]{:S(2)}) copy-start(f32[768]{0:T(1024)S(1)} %get-tuple-element.69) | copy-start | bytes 9220
  72.7 14.6 %copy-start.303 = (f32[512]{0:T(512)}, f32[512]{0:T(512)S(1)}, u32[]{:S(2)}) copy-start(f32[512]{0:T(512)S(1)} %broadcast_multiply_fusion.9) | copy-start | bytes 6148
  73.1 14.2 %copy-start.403 = (f32[512]{0:T(512)}, f32[512]{0:T(512)S(1)}, u32[]{:S(2)}) copy-start(f32[512]{0:T(512)S(1)} %add_rsqrt_fusion.3) | copy-start | bytes 6148
  74.0 18.2 %collective-permute-start.4 = (bf16[2304,768]{1,0:T(8,128)(2,1)}, bf16[2304,768]{1,0:T(8,128)(2,1)}, u32[]{:S(2)}, u32[]{:S(2)}) collective-permute-start(bf16[2304,768]{1,0:T(8,128)(2,1)} %pad_maximum_fusion.4), channel_id=1, source_target_pairs={{1,3},{3,1},{5,7},{7,5},{9,11},{11,9},{13,15},{15,13},{17,19},{19,... | collective-permute-start | bytes 10616840 | tf_op jit(solution)/shard_map/ppermute | solution.py:209
  84.2 16.3 %copy-start.79 = (bf16[2304,768]{1,0:T(8,128)(2,1)}, bf16[2304,768]{1,0:T(8,128)(2,1)S(1)}, u32[]{:S(2)}) copy-start(bf16[2304,768]{1,0:T(8,128)(2,1)S(1)} %get-tuple-element.141) | copy-start | bytes 10616836
  85.8 8.1 %collective-permute-start.3 = (bf16[512,384]{0,1:T(8,128)(2,1)S(1)}, bf16[512,384]{0,1:T(8,128)(2,1)S(1)}, u32[]{:S(2)}, u32[]{:S(2)}) collective-permute-start(bf16[512,384]{0,1:T(8,128)(2,1)S(1)} %pad_maximum_fusion.28), channel_id=1, source_target_pairs={{0,1},{1,0},{2,3},{3,2},{4,5},{5,4},{6,7},{7,6},{8,9},{9,8},{10,11... | collective-permute-start | bytes 1179656 | tf_op jit(solution)/shard_map/ppermute | solution.py:237
  92.3 39.5 %collective-permute-start.5 = (bf16[2304,768]{1,0:T(8,128)(2,1)}, bf16[2304,768]{1,0:T(8,128)(2,1)}, u32[]{:S(2)}, u32[]{:S(2)}) collective-permute-start(bf16[2304,768]{1,0:T(8,128)(2,1)} %collective-permute-done.4), channel_id=1, source_target_pairs={{3,2},{1,0},{7,6},{5,4},{11,10},{9,8},{15,14},{13,12},{19,18},{17,... | collective-permute-start | bytes 10616840 | tf_op jit(solution)/shard_map/ppermute | solution.py:212
  126.6 38.4 %copy-start.277 = (f32[512]{0:T(512)}, f32[512]{0:T(512)S(1)}, u32[]{:S(2)}) copy-start(f32[512]{0:T(512)S(1)} %broadcast_multiply_fusion.8) | copy-start | bytes 6148
  131.7 33.3 %copy-start.305 = (f32[512]{0:T(512)}, f32[512]{0:T(512)S(1)}, u32[]{:S(2)}) copy-start(f32[512]{0:T(512)S(1)} %add_rsqrt_fusion.2) | copy-start | bytes 6148
  137.3 32.8 %copy-start.85 = (bf16[2304,768]{1,0:T(8,128)(2,1)}, bf16[2304,768]{1,0:T(8,128)(2,1)S(1)}, u32[]{:S(2)}) copy-start(bf16[2304,768]{1,0:T(8,128)(2,1)S(1)} %get-tuple-element.144) | copy-start | bytes 10616836
  137.3 43.0 %copy-start.81 = (bf16[2304,768]{1,0:T(8,128)(2,1)}, bf16[2304,768]{1,0:T(8,128)(2,1)S(1)}, u32[]{:S(2)}) copy-start(bf16[2304,768]{1,0:T(8,128)(2,1)S(1)} %get-tuple-element.143) | copy-start | bytes 10616836
  139.3 25.7 %copy-start.349 = (f32[768]{0:T(1024)S(1)}, f32[768]{0:T(1024)}, u32[]{:S(2)}) copy-start(f32[768]{0:T(1024)} %get-tuple-element.63) | copy-start | bytes 9220
  139.3 25.7 %copy-start.352 = (f32[768]{0:T(1024)S(1)}, f32[768]{0:T(1024)}, u32[]{:S(2)}) copy-start(f32[768]{0:T(1024)} %get-tuple-element.62) | copy-start | bytes 9220
  139.3 25.7 %copy-start.372 = (f32[768]{0:T(1024)S(1)}, f32[768]{0:T(1024)}, u32[]{:S(2)}) copy-start(f32[768]{0:T(1024)} %get-tuple-element.61) | copy-start | bytes 9220
  139.7 36.3 %copy-start.120 = (bf16[512,384]{0,1:T(8,128)(2,1)}, bf16[512,384]{0,1:T(8,128)(2,1)S(1)}, u32[]{:S(2)}) copy-start(bf16[512,384]{0,1:T(8,128)(2,1)S(1)} %fusion.152) | copy-start | bytes 1179652
  139.8 31.4 %collective-permute-start.6 = (bf16[512,384]{0,1:T(8,128)(2,1)S(1)}, bf16[512,384]{0,1:T(8,128)(2,1)S(1)}, u32[]{:S(2)}, u32[]{:S(2)}) collective-permute-start(bf16[512,384]{0,1:T(8,128)(2,1)S(1)} %pad_maximum_fusion.29), channel_id=1, source_target_pairs={{0,1},{1,0},{2,3},{3,2},{4,5},{5,4},{6,7},{7,6},{8,9},{9,8},{10,11... | collective-permute-start | bytes 1179656 | tf_op jit(solution)/shard_map/ppermute | solution.py:237
  180.4 39.1 %copy-start.262 = (bf16[256,64]{0,1:T(8,128)(2,1)}, bf16[256,64]{0,1:T(8,128)(2,1)S(1)}, u32[]{:S(2)}) copy-start(bf16[256,64]{0,1:T(8,128)(2,1)S(1)} %convolution_convert_fusion.65) | copy-start | bytes 98308
  225.3 12.2 %copy-start.122 = (bf16[512,384]{0,1:T(8,128)(2,1)}, bf16[512,384]{0,1:T(8,128)(2,1)S(1)}, u32[]{:S(2)}) copy-start(bf16[512,384]{0,1:T(8,128)(2,1)S(1)} %fusion.151) | copy-start | bytes 1179652
  225.4 7.7 collective-permute-start.7
  286.9 39.7 %copy-start.285 = (f32[512]{0:T(512)}, f32[512]{0:T(512)S(1)}, u32[]{:S(2)}) copy-start(f32[512]{0:T(512)S(1)} %broadcast_multiply_fusion.6) | copy-start | bytes 6148
  288.6 38.0 %copy-start.313 = (f32[512]{0:T(512)}, f32[512]{0:T(512)S(1)}, u32[]{:S(2)}) copy-start(f32[512]{0:T(512)S(1)} %add_rsqrt_fusion) | copy-start | bytes 6148
  294.5 103.9 %copy-start.6 = (f32[768,768]{1,0:T(8,128)}, f32[768,768]{1,0:T(8,128)S(1)}, u32[]{:S(2)}) copy-start(f32[768,768]{1,0:T(8,128)S(1)} %fusion.260) | copy-start | bytes 7077892
  299.2 3.1 collective-permute-start.8
  318.4 3.6 collective-permute-start.9
  398.3 12.6 %collective-permute-start.10 = (f32[512,384]{0,1:T(8,128)}, f32[512,384]{0,1:T(8,128)}, u32[]{:S(2)}, u32[]{:S(2)}) collective-permute-start(f32[512,384]{0,1:T(8,128)} %pad_maximum_fusion.17), channel_id=1, source_target_pairs={{0,1},{1,0},{2,3},{3,2},{4,5},{5,4},{6,7},{7,6},{8,9},{9,8},{10,11... | collective-permute-start | bytes 2359304 | tf_op jit(solution)/shard_map/ppermute | solution.py:268
  400.6 242.1 %collective-permute-start.19 = (bf16[2304,768]{1,0:T(8,128)(2,1)}, bf16[2304,768]{1,0:T(8,128)(2,1)}, u32[]{:S(2)}, u32[]{:S(2)}) collective-permute-start(bf16[2304,768]{1,0:T(8,128)(2,1)} %fusion.154), channel_id=1, source_target_pairs={{2,3},{0,1},{6,7},{4,5},{10,11},{8,9},{14,15},{12,13},{18,19},{16,... | collective-permute-start | bytes 10616840 | tf_op jit(solution)/shard_map/ppermute | solution.py:282
  484.5 10.6 %collective-permute-start.11 = (f32[512,384]{0,1:T(8,128)}, f32[512,384]{0,1:T(8,128)}, u32[]{:S(2)}, u32[]{:S(2)}) collective-permute-start(f32[512,384]{0,1:T(8,128)} %pad_maximum_fusion.20), channel_id=1, source_target_pairs={{0,1},{1,0},{2,3},{3,2},{4,5},{5,4},{6,7},{7,6},{8,9},{9,8},{10,11... | collective-permute-start | bytes 2359304 | tf_op jit(solution)/shard_map/ppermute | solution.py:268
  486.6 164.7 %collective-permute-start.17 = (bf16[2304,768]{1,0:T(8,128)(2,1)}, bf16[2304,768]{1,0:T(8,128)(2,1)}, u32[]{:S(2)}, u32[]{:S(2)}) collective-permute-start(bf16[2304,768]{1,0:T(8,128)(2,1)} %fusion.155), channel_id=1, source_target_pairs={{3,2},{1,0},{7,6},{5,4},{11,10},{9,8},{15,14},{13,12},{19,18},{17,... | collective-permute-start | bytes 10616840 | tf_op jit(solution)/shard_map/ppermute | solution.py:282
  572.1 16.1 %collective-permute-start.12 = (f32[512,384]{0,1:T(8,128)}, f32[512,384]{0,1:T(8,128)}, u32[]{:S(2)}, u32[]{:S(2)}) collective-permute-start(f32[512,384]{0,1:T(8,128)} %pad_maximum_fusion.23), channel_id=1, source_target_pairs={{0,1},{1,0},{2,3},{3,2},{4,5},{5,4},{6,7},{7,6},{8,9},{9,8},{10,11... | collective-permute-start | bytes 2359304 | tf_op jit(solution)/shard_map/ppermute | solution.py:268
  575.0 85.8 %collective-permute-start.15 = (bf16[2304,768]{1,0:T(8,128)(2,1)}, bf16[2304,768]{1,0:T(8,128)(2,1)}, u32[]{:S(2)}, u32[]{:S(2)}) collective-permute-start(bf16[2304,768]{1,0:T(8,128)(2,1)} %fusion.156), channel_id=1, source_target_pairs={{0,1},{2,3},{4,5},{6,7},{8,9},{10,11},{12,13},{14,15},{16,17},{18,... | collective-permute-start | bytes 10616840 | tf_op jit(solution)/shard_map/ppermute | solution.py:282
  594.8 108.0 %all-gather.4.cloned.1.call-start = ((), (), s32[]{:S(2)}) async-start(), calls=%async_computation.1 | async-start | bytes 3932160 | tf_op jit(solution)/shard_map/all_gather | solution.py:246
  600.6 66.7 %collective-permute-start.13 = (bf16[2304,768]{1,0:T(8,128)(2,1)}, bf16[2304,768]{1,0:T(8,128)(2,1)}, u32[]{:S(2)}, u32[]{:S(2)}) collective-permute-start(bf16[2304,768]{1,0:T(8,128)(2,1)} %fusion.157), channel_id=1, source_target_pairs={{1,0},{3,2},{5,4},{7,6},{9,8},{11,10},{13,12},{15,14},{17,16},{19,... | collective-permute-start | bytes 10616840 | tf_op jit(solution)/shard_map/ppermute | solution.py:282
  601.9 40.8 %copy-start.61 = (f32[192,768]{1,0:T(8,128)S(1)}, f32[192,768]{1,0:T(8,128)}, u32[]{:S(2)}) copy-start(f32[192,768]{1,0:T(8,128)} %fusion.894) | copy-start | bytes 1769476
  648.7 12.1 %copy-start.21 = (f32[576,768]{1,0:T(8,128)S(1)}, f32[576,768]{1,0:T(8,128)}, u32[]{:S(2)}) copy-start(f32[576,768]{1,0:T(8,128)} %copy-done.20) | copy-start | bytes 5308420
  648.7 12.1 %copy-start.65 = (f32[192,768]{1,0:T(8,128)S(1)}, f32[192,768]{1,0:T(8,128)}, u32[]{:S(2)}) copy-start(f32[192,768]{1,0:T(8,128)} %fusion.896) | copy-start | bytes 1769476
  648.7 58.6 %collective-permute-start.20 = (bf16[2304,768]{1,0:T(8,128)(2,1)}, bf16[2304,768]{1,0:T(8,128)(2,1)}, u32[]{:S(2)}, u32[]{:S(2)}) collective-permute-start(bf16[2304,768]{1,0:T(8,128)(2,1)} %fusion.3), channel_id=1, source_target_pairs={{1,3},{5,7},{9,11},{13,15},{17,19},{21,23},{25,27},{29,31}} | collective-permute-start | bytes 10616840 | tf_op jit(solution)/shard_map/ppermute | solution.py:284
  655.3 12.0 %copy-start.67 = (f32[192,768]{1,0:T(8,128)S(1)}, f32[192,768]{1,0:T(8,128)}, u32[]{:S(2)}) copy-start(f32[192,768]{1,0:T(8,128)} %fusion.897) | copy-start | bytes 1769476
  655.3 90.7 %collective-permute-start.18 = (bf16[2304,768]{1,0:T(8,128)(2,1)}, bf16[2304,768]{1,0:T(8,128)(2,1)}, u32[]{:S(2)}, u32[]{:S(2)}) collective-permute-start(bf16[2304,768]{1,0:T(8,128)(2,1)} %fusion.2), channel_id=1, source_target_pairs={{0,2},{4,6},{8,10},{12,14},{16,18},{20,22},{24,26},{28,30}} | collective-permute-start | bytes 10616840 | tf_op jit(solution)/shard_map/ppermute | solution.py:284
  664.8 81.2 %collective-permute-start.16 = (bf16[2304,768]{1,0:T(8,128)(2,1)}, bf16[2304,768]{1,0:T(8,128)(2,1)}, u32[]{:S(2)}, u32[]{:S(2)}) collective-permute-start(bf16[2304,768]{1,0:T(8,128)(2,1)} %fusion.1), channel_id=1, source_target_pairs={{3,1},{7,5},{11,9},{15,13},{19,17},{23,21},{27,25},{31,29}} | collective-permute-start | bytes 10616840 | tf_op jit(solution)/shard_map/ppermute | solution.py:284
  671.1 81.4 %collective-permute-start.14 = (bf16[2304,768]{1,0:T(8,128)(2,1)}, bf16[2304,768]{1,0:T(8,128)(2,1)}, u32[]{:S(2)}, u32[]{:S(2)}) collective-permute-start(bf16[2304,768]{1,0:T(8,128)(2,1)} %fusion), channel_id=1, source_target_pairs={{2,0},{6,4},{10,8},{14,12},{18,16},{22,20},{26,24},{30,28}} | collective-permute-start | bytes 10616840 | tf_op jit(solution)/shard_map/ppermute | solution.py:284
  673.9 98.0 %copy-start.302 = (f32[1,768]{1,0:T(1,128)}, f32[1,768]{1,0:T(1,128)S(1)}, u32[]{:S(2)}) copy-start(f32[1,768]{1,0:T(1,128)S(1)} %get-tuple-element.340) | copy-start | bytes 9220
  702.8 49.7 %copy-start.68 = (f32[192,768]{1,0:T(8,128)S(1)}, f32[192,768]{1,0:T(8,128)}, u32[]{:S(2)}) copy-start(f32[192,768]{1,0:T(8,128)} %fusion.897) | copy-start | bytes 1769476
  704.9 47.6 %copy-start.7 = (f32[768,768]{1,0:T(8,128)S(1)}, f32[768,768]{1,0:T(8,128)}, u32[]{:S(2)}) copy-start(f32[768,768]{1,0:T(8,128)} %copy-done.6) | copy-start | bytes 7077892
  704.9 47.6 %copy-start.9 = (f32[768,768]{1,0:T(8,128)S(1)}, f32[768,768]{1,0:T(8,128)}, u32[]{:S(2)}) copy-start(f32[768,768]{1,0:T(8,128)} %fusion.465) | copy-start | bytes 7077892
  704.9 47.6 %copy-start.12 = (f32[768,768]{1,0:T(8,128)S(1)}, f32[768,768]{1,0:T(8,128)}, u32[]{:S(2)}) copy-start(f32[768,768]{1,0:T(8,128)} %fusion.462) | copy-start | bytes 7077892
  705.4 47.2 %copy-start.2 = (f32[768,768]{1,0:T(8,128)S(1)}, f32[768,768]{1,0:T(8,128)}, u32[]{:S(2)}) copy-start(f32[768,768]{1,0:T(8,128)} %fusion.258) | copy-start | bytes 7077892
  705.4 47.2 %copy-start.5 = (f32[768,768]{1,0:T(8,128)S(1)}, f32[768,768]{1,0:T(8,128)}, u32[]{:S(2)}) copy-start(f32[768,768]{1,0:T(8,128)} %fusion.257) | copy-start | bytes 7077892
  705.4 47.2 %copy-start.66 = (f32[192,768]{1,0:T(8,128)S(1)}, f32[192,768]{1,0:T(8,128)}, u32[]{:S(2)}) copy-start(f32[192,768]{1,0:T(8,128)} %fusion.896) | copy-start | bytes 1769476
  (377 other events, 1111.7 us)
Sparse Core Ops, SparseCore 0:
  594.9 37.5 all-reduce.6
  642.7 48.1 all-gather.3

commit v2 on v1

v2 whole, which is shorter than its diff:
```python
import functools

import jax
import jax.numpy as jnp
from jax import lax
from jax.experimental import pallas as pl
from jax.experimental.pallas import tpu as pltpu
from jax.sharding import PartitionSpec as P

BF = jnp.bfloat16
F32 = jnp.float32
ROPE_BASE = 10000.0
LN_EPS = 1e-5
HEADS = 3
HEAD = 64
PART = HEADS * HEAD
BLOCK = 256
ROWS = 2 * BLOCK
STAGE_SPECS = (P('pp', None), P('pp', None), P('pp', None, 'tp', None, None), P('pp', 'tp', None, None), P('pp', 'tp', None, None), P('pp', None), P('pp', None), P('pp', None), P('pp', None, 'tp'), P('pp', 'tp'), P('pp', 'tp', None), P('pp', None))
GRAD_SPECS = (P(('dp', 'pp'), None), P(('dp', 'pp'), None), P(('dp', 'pp'), None, 'tp', None, None), P(('dp', 'pp'), 'tp', None, None), P(('dp', 'pp'), 'tp', None, None), P(('dp', 'pp'), None), P(('dp', 'pp'), None), P(('dp', 'pp'), None), P(('dp', 'pp'), None, 'tp'), P(('dp', 'pp'), 'tp'), P(('dp', 'pp'), 'tp', None), P(('dp', 'pp'), None))
CHUNKS = 8
LIMIT = 60 * 2 ** 20
MESH_ID = pl.DeviceIdType.MESH


def tie(*values):
    return lax.optimization_barrier(values)


def dot(left, right, left_dim, right_dim):
    return lax.dot_general(left, right, (((left_dim,), (right_dim,)), ((), ())), preferred_element_type=F32)


def normalise(hidden):
    hidden_f = hidden.astype(F32)
    center = hidden_f - jnp.mean(hidden_f, axis=-1, keepdims=True)
    scale = lax.rsqrt(jnp.mean(center * center, axis=-1, keepdims=True) + LN_EPS)
    return center * scale, scale


def turn_matrix(width, transposed):
    row = lax.broadcasted_iota(jnp.int32, (width, width), 0)
    col = lax.broadcasted_iota(jnp.int32, (width, width), 1)
    if transposed:
        row, col = col, row
    dim = col % HEAD
    minus = (dim < 8) & (row == col + 8)
    plus = (dim >= 8) & (dim < 16) & (row == col - 8)
    return (plus.astype(F32) - minus.astype(F32)).astype(BF)


def rotate_head(values, cos_tab, sin_tab, transposed):
    turned = dot(values, turn_matrix(HEAD, transposed), 1, 0)
    return (values.astype(F32) * cos_tab + turned * sin_tab).astype(BF)


def block_rows(block):
    return slice(block * BLOCK, (block + 1) * BLOCK)


def pick_weights(stage, options, first, count, scratch, sem):
    for index, option in enumerate(options):
        @pl.when(stage == index)
        def fetch():
            pltpu.make_async_copy(option.at[pl.ds(first, count)], scratch, sem).start()

    return pltpu.make_async_copy(options[0].at[pl.ds(first, count)], scratch, sem).wait


def meet(n_tp, with_sum, with_core):
    rank, stage = lax.axis_index('tp'), lax.axis_index('pp')
    barrier = pltpu.get_barrier_semaphore()
    count = 0
    if with_core:
        pl.semaphore_signal(barrier, inc=1, device_id={'pp': stage + 1 - 2 * lax.rem(stage, 2)}, device_id_type=MESH_ID)
        count = 1
    if with_sum:
        is_inner = lax.rem((rank + 1) // 2, 2)
        near = rank + 1 - 2 * lax.rem(rank, 2)
        pl.semaphore_signal(barrier, inc=1, device_id={'tp': near}, device_id_type=MESH_ID)

        @pl.when(is_inner == 1)
        def greet():
            pl.semaphore_signal(barrier, inc=1, device_id={'tp': n_tp - 1 - rank}, device_id_type=MESH_ID)

        count = count + 1 + is_inner
    pl.semaphore_wait(barrier, count)


class LineSum:
    def __init__(self, n_tp, part, base, out, inbox, half, across, sems):
        self.part, self.base, self.out, self.inbox, self.half, self.across, self.sems = part, base, out, inbox, half, across, sems
        rank = lax.axis_index('tp')
        self.is_inner = lax.rem((rank + 1) // 2, 2)
        self.near = rank + 1 - 2 * lax.rem(rank, 2)
        self.mirror = n_tp - 1 - rank
        self.n_chunks = CHUNKS
        self.size = out.shape[0] // CHUNKS

    def span(self, chunk):
        return pl.ds(chunk * self.size, self.size)

    def copy(self, kind, chunk):
        source, target, device = ((self.part, self.inbox, self.near), (self.half, self.across, self.mirror), (self.out, self.out, self.near))[kind]
        return pltpu.make_async_remote_copy(
            src_ref=source.at[self.span(chunk)], dst_ref=target.at[self.span(chunk)], send_sem=self.sems[2 * kind].at[chunk],
            recv_sem=self.sems[2 * kind + 1].at[chunk], device_id={'tp': device}, device_id_type=MESH_ID)

    def offer(self, chunks):
        @pl.when(self.is_inner == 0)
        def start():
            for chunk in chunks:
                self.copy(0, chunk).start()

    def finish(self, chunk):
        rows = self.span(chunk)
        self.copy(1, chunk).wait_recv()
        both = self.half[rows, :].astype(F32) + self.across[rows, :].astype(F32)
        self.out[rows, :] = (self.base(rows) + both).astype(BF)
        self.copy(2, chunk).start()

    def step(self, chunk):
        @pl.when(self.is_inner == 1)
        def merge():
            rows = self.span(chunk)
            self.copy(0, chunk).wait_recv()
            self.half[rows, :] = (self.part[rows, :].astype(F32) + self.inbox[rows, :].astype(F32)).astype(BF)
            self.copy(1, chunk).start()

    def close(self, chunk):
        @pl.when(self.is_inner == 1)
        def end():
            self.finish(chunk)

    def drain(self):
        @pl.when(self.is_inner == 1)
        def inner_end():
            for chunk in range(self.n_chunks):
                self.copy(1, chunk).wait_send()
                self.copy(2, chunk).wait_send()

        @pl.when(self.is_inner == 0)
        def outer_end():
            for chunk in range(self.n_chunks):
                self.copy(2, chunk).wait_recv()
                self.copy(0, chunk).wait_send()


def line_scratch(rows, width):
    return [pltpu.VMEM((rows, width), BF)] * 3 + [pltpu.SemaphoreType.DMA((CHUNKS,))] * 6


def forward_kernel(n_tp, with_sum, h_ref, opt0, opt1, opt2, opt3, vec_ref, bq_ref, cos_ref, sin_ref,
                   out_ref, q_ref, kv_ref, ctx_ref, lse_ref, pre_ref, weights, w_sem, active, kv_send, kv_recv, *line_refs):
    stage = lax.axis_index('pp')
    core = lax.rem(stage, 2)
    width = h_ref.shape[1]
    wait_weights = pick_weights(stage, (opt0, opt1, opt2, opt3), 0, weights.shape[0], weights, w_sem)
    meet(n_tp, with_sum, True)
    wait_weights()

    def project(normed, index):
        return (dot(normed, weights[index * HEAD:(index + 1) * HEAD, :], 1, 1) + bq_ref[index:index + 1, :]).astype(BF)

    swaps = []
    for block in range(2):
        rows = block_rows(block)
        xhat, _ = normalise(h_ref[rows, :])
        normed_a = (xhat * vec_ref[0:1, :] + vec_ref[1:2, :]).astype(BF)
        active[rows, :] = (xhat * vec_ref[2:3, :] + vec_ref[3:4, :]).astype(BF)
        cos_tab, sin_tab = cos_ref[rows, :], sin_ref[rows, :]
        place = slice(2 * block * BLOCK, (2 * block + 1) * BLOCK)
        for head in range(HEADS):
            q_ref[head, rows, :] = rotate_head(project(normed_a, head), cos_tab, sin_tab, False)
            kv_ref[head, place, :] = rotate_head(project(normed_a, HEADS + head), cos_tab, sin_tab, False)
            kv_ref[HEADS + head, place, :] = project(normed_a, 2 * HEADS + head)
        copy = pltpu.make_async_remote_copy(
            src_ref=kv_ref.at[:, pl.ds(2 * block * BLOCK, BLOCK), :], dst_ref=kv_ref.at[:, pl.ds((2 * block + 1) * BLOCK, BLOCK), :],
            send_sem=kv_send.at[block], recv_sem=kv_recv.at[block],
            device_id={'pp': stage + 1 - 2 * core}, device_id_type=MESH_ID)
        copy.start()
        swaps.append(copy)
    for block in range(2):
        rows = block_rows(block)
        pre_act = dot(active[rows, :], weights[4 * PART:4 * PART + width, :], 1, 0) + vec_ref[5:6, :]
        pre_ref[rows, :] = pre_act
        active[rows, :] = (0.5 * pre_act * (1.0 + lax.erf(pre_act * (2.0 ** -0.5)))).astype(BF)
    for copy in swaps:
        copy.wait_recv()
    if with_sum:
        part_ref = line_refs[0]
        line = LineSum(n_tp, part_ref, lambda rows: h_ref[rows, :].astype(F32) + vec_ref[4:5, :], out_ref, *line_refs[1:4], line_refs[4:])
    else:
        part_ref = out_ref
    for block in range(2):
        rows = block_rows(block)
        n_keys = (2, 4)[block] * BLOCK
        mask = causal_mask(core, block, n_keys)
        part = dot(active[rows, :], weights[4 * PART + width:, :], 1, 0)
        for head in range(HEADS):
            scores = dot(q_ref[head, rows, :], kv_ref[head, :n_keys, :], 1, 1) * (HEAD ** -0.5)
            scores = jnp.where(mask, scores, -1e30)
            top = jnp.max(scores, axis=-1, keepdims=True)
            expo = jnp.exp(scores - top)
            total = jnp.sum(expo, axis=-1, keepdims=True)
            probs = (expo / total).astype(BF)
            context = dot(probs, kv_ref[HEADS + head, :n_keys, :], 1, 0).astype(BF)
            ctx_ref[head, rows, :] = context
            lse_ref[head, rows, :] = top + jnp.log(total)
            part += dot(context, weights[3 * PART + head * HEAD:3 * PART + (head + 1) * HEAD, :], 1, 0)
        part_ref[rows, :] = part.astype(BF)
        if with_sum:
            line.offer(range(block * CHUNKS // 2, (block + 1) * CHUNKS // 2))
    if with_sum:
        for chunk in range(CHUNKS):
            line.step(chunk)
            if chunk:
                line.close(chunk - 1)
        line.close(CHUNKS - 1)
        line.drain()
    for copy in swaps:
        copy.wait_send()


def forward_layer(hidden, options, vec, bias_q, cos_tab, sin_tab, n_tp, with_sum):
    rows, width = hidden.shape
    block, anywhere = pl.BlockSpec(memory_space=pltpu.VMEM), pl.BlockSpec(memory_space=pl.ANY)
    scratch = [pltpu.VMEM(options[0].shape, BF), pltpu.SemaphoreType.DMA, pltpu.VMEM((rows, width), BF), pltpu.SemaphoreType.DMA((2,)), pltpu.SemaphoreType.DMA((2,))]
    if with_sum:
        scratch += [pltpu.VMEM((rows, width), BF)] + line_scratch(rows, width)
    return pl.pallas_call(
        functools.partial(forward_kernel, n_tp, with_sum),
        out_shape=(jax.ShapeDtypeStruct((rows, width), BF), jax.ShapeDtypeStruct((HEADS, rows, HEAD), BF), jax.ShapeDtypeStruct((2 * HEADS, 2 * rows, HEAD), BF),
                   jax.ShapeDtypeStruct((HEADS, rows, HEAD), BF), jax.ShapeDtypeStruct((HEADS, rows, 1), F32), jax.ShapeDtypeStruct((rows, width), F32)),
        in_specs=[block] + [anywhere] * 4 + [block] * 4,
        out_specs=tuple([block] * 6),
        scratch_shapes=scratch,
        compiler_params=pltpu.CompilerParams(collective_id=0 if with_sum else 1, has_side_effects=True, vmem_limit_bytes=LIMIT),
        cost_estimate=pl.CostEstimate(flops=40_000_000_000, bytes_accessed=8_000_000, transcendentals=0),
    )(hidden, *options, vec, bias_q, cos_tab, sin_tab)


def mlp_back_kernel(g_ref, h_ref, pre_ref, opt0, opt1, opt2, opt3, vec_ref, gx_ref, prod_ref, prod_b_ref, small_ref,
                    weights, w_sem, normed, gpre, active):
    stage = lax.axis_index('pp')
    width = h_ref.shape[1]
    wait_weights = pick_weights(stage, (opt0, opt1, opt2, opt3), 4 * PART, weights.shape[0], weights, w_sem)
    wait_weights()
    sums = [0.0] * 4
    for block in range(2):
        rows = block_rows(block)
        grad = g_ref[rows, :]
        pre_act = pre_ref[rows, :]
        gauss = 0.5 * (1.0 + lax.erf(pre_act * (2.0 ** -0.5)))
        active[rows, :] = (pre_act * gauss).astype(BF)
        slope = gauss + pre_act * jnp.exp(-0.5 * pre_act * pre_act) * 0.3989422804014327
        grad_pre = dot(grad, weights[width:, :], 1, 1) * slope
        gpre[rows, :] = grad_pre.astype(BF)
        sums[3] += jnp.sum(grad_pre, axis=0, keepdims=True)
        sums[2] += jnp.sum(grad.astype(F32), axis=0, keepdims=True)
        xhat, _ = normalise(h_ref[rows, :])
        normed[rows, :] = (xhat * vec_ref[2:3, :] + vec_ref[3:4, :]).astype(BF)
        grad_m = dot(gpre[rows, :], weights[:width, :], 1, 1)
        sums[0] += jnp.sum(grad_m * xhat, axis=0, keepdims=True)
        sums[1] += jnp.sum(grad_m, axis=0, keepdims=True)
        gx_ref[rows, :] = grad_m * vec_ref[2:3, :]
    for index, value in enumerate(sums):
        small_ref[index:index + 1, :] = value
    for first in range(0, width, 256):
        for left, right, row in ((normed, gpre, 0), (active, g_ref, width)):
            value = dot(left[:, first:first + 256], right[...], 0, 0)
            prod_ref[row + first:row + first + 256, :] = value
            prod_b_ref[row + first:row + first + 256, :] = value.astype(BF)


def mlp_back(grad, hidden, pre_act, options, vec):
    rows, width = hidden.shape
    block, anywhere = pl.BlockSpec(memory_space=pltpu.VMEM), pl.BlockSpec(memory_space=pl.ANY)
    return pl.pallas_call(
        mlp_back_kernel,
        out_shape=(jax.ShapeDtypeStruct((rows, width), F32), jax.ShapeDtypeStruct((2 * width, width), F32), jax.ShapeDtypeStruct((2 * width, width), BF), jax.ShapeDtypeStruct((4, width), F32)),
        in_specs=[block] * 3 + [anywhere] * 4 + [block],
        out_specs=tuple([block] * 4),
        scratch_shapes=[pltpu.VMEM((2 * width, width), BF), pltpu.SemaphoreType.DMA] + [pltpu.VMEM((rows, width), BF)] * 3,
        compiler_params=pltpu.CompilerParams(vmem_limit_bytes=LIMIT),
        cost_estimate=pl.CostEstimate(flops=10_000_000_000, bytes_accessed=12_000_000, transcendentals=0),
    )(grad, hidden, pre_act, *options, vec)


def att_back_kernel(n_tp, with_sum, g_ref, h_ref, gx_ref, q_ref, kv_ref, ctx_ref, lse_ref, opt0, opt1, opt2, opt3, vec_ref, cos_ref, sin_ref, *refs):
    if with_sum:
        out_ref, prod_ref, prod_b_ref, small_ref, bq_ref = refs[:5]
        refs = refs[5:]
    else:
        prod_ref, prod_b_ref, small_ref, bq_ref = refs[:4]
        refs = refs[4:]
    weights, w_sem, dkv, landed, dqkv, normed, kv_send, kv_recv = refs[:8]
    line_refs = refs[8:]
    stage = lax.axis_index('pp')
    core = lax.rem(stage, 2)
    wait_weights = pick_weights(stage, (opt0, opt1, opt2, opt3), 0, weights.shape[0], weights, w_sem)
    meet(n_tp, with_sum, True)
    wait_weights()
    for block in (1, 0):
        rows = block_rows(block)
        n_keys = (2, 4)[block] * BLOCK
        mask = causal_mask(core, block, n_keys)
        for head in range(HEADS):
            d_ctx = dot(g_ref[rows, :], weights[3 * PART + head * HEAD:3 * PART + (head + 1) * HEAD, :], 1, 1).astype(BF)
            q_part = q_ref[head, rows, :]
            k_part = kv_ref[head, :n_keys, :]
            scores = dot(q_part, k_part, 1, 1) * (HEAD ** -0.5)
            probs = jnp.where(mask, jnp.exp(scores - lse_ref[head, rows, :]), 0.0)
            dprobs = dot(d_ctx, kv_ref[HEADS + head, :n_keys, :], 1, 1).astype(BF).astype(F32)
            delta = jnp.sum(probs * dprobs, axis=-1, keepdims=True)
            dscores = (probs * (dprobs - delta) * (HEAD ** -0.5)).astype(BF)
            dqkv[head, rows, :] = dot(dscores, k_part, 1, 0).astype(BF)
            d_k = dot(dscores, q_part, 0, 0)
            d_v = dot(probs.astype(BF), d_ctx, 0, 0)
            if block == 1:
                dkv[head] = d_k
                dkv[HEADS + head] = d_v
            else:
                dkv[head, :n_keys, :] += d_k
                dkv[HEADS + head, :n_keys, :] += d_v
    swaps = []
    for block in range(2):
        copy = pltpu.make_async_remote_copy(
            src_ref=dkv.at[:, pl.ds((2 * block + 1) * BLOCK, BLOCK), :], dst_ref=landed.at[:, pl.ds(block * BLOCK, BLOCK), :],
            send_sem=kv_send.at[block], recv_sem=kv_recv.at[block],
            device_id={'pp': stage + 1 - 2 * core}, device_id_type=MESH_ID)
        copy.start()
        swaps.append(copy)
    if with_sum:
        part_ref = line_refs[0]
        line = LineSum(n_tp, part_ref, lambda rows: g_ref[rows, :].astype(F32), out_ref, *line_refs[1:4], line_refs[4:])
    sums = [0.0] * 2
    bias = [0.0] * (3 * HEADS)
    for copy in swaps:
        copy.wait_recv()
    for block in range(2):
        rows = block_rows(block)
        own = slice(2 * block * BLOCK, (2 * block + 1) * BLOCK)
        cos_tab, sin_tab = cos_ref[rows, :], sin_ref[rows, :]
        grad_a = 0.0
        for head in range(HEADS):
            d_q = rotate_head(dqkv[head, rows, :], cos_tab, sin_tab, True)
            d_k = rotate_head((dkv[head, own, :] + landed[head, rows, :]).astype(BF), cos_tab, sin_tab, True)
            d_v = (dkv[HEADS + head, own, :] + landed[HEADS + head, rows, :]).astype(BF)
            for kind, value in enumerate((d_q, d_k, d_v)):
                index = kind * HEADS + head
                dqkv[index, rows, :] = value
                bias[index] += jnp.sum(value.astype(F32), axis=0, keepdims=True)
                grad_a += dot(value, weights[index * HEAD:(index + 1) * HEAD, :], 1, 0)
        xhat, scale = normalise(h_ref[rows, :])
        normed[rows, :] = (xhat * vec_ref[0:1, :] + vec_ref[1:2, :]).astype(BF)
        sums[0] += jnp.sum(grad_a * xhat, axis=0, keepdims=True)
        sums[1] += jnp.sum(grad_a, axis=0, keepdims=True)
        if with_sum:
            grad_x = grad_a * vec_ref[0:1, :] + gx_ref[rows, :]
            branch = scale * (grad_x - jnp.mean(grad_x, axis=-1, keepdims=True) - xhat * jnp.mean(grad_x * xhat, axis=-1, keepdims=True))
            part_ref[rows, :] = branch.astype(BF)
            line.offer(range(block * CHUNKS // 2, (block + 1) * CHUNKS // 2))
    for index, value in enumerate(sums):
        small_ref[index:index + 1, :] = value
    for index, value in enumerate(bias):
        bq_ref[index:index + 1, :] = value

    def product(index):
        value = dot(dqkv[index], normed[...], 0, 0) if index < 3 * HEADS else dot(ctx_ref[index - 3 * HEADS], g_ref[...], 0, 0)
        prod_ref[index * HEAD:(index + 1) * HEAD, :] = value
        prod_b_ref[index * HEAD:(index + 1) * HEAD, :] = value.astype(BF)

    n_prod = 4 * HEADS
    for chunk in range(CHUNKS):
        if with_sum:
            line.step(chunk)
        for index in range(chunk * n_prod // CHUNKS, (chunk + 1) * n_prod // CHUNKS):
            product(index)
        if with_sum and chunk:
            line.close(chunk - 1)
    if with_sum:
        line.close(CHUNKS - 1)
        line.drain()
    for copy in swaps:
        copy.wait_send()


def att_back(grad, hidden, gx, query, kv_all, context, lse, options, vec, cos_tab, sin_tab, n_tp, with_sum):
    rows, width = hidden.shape
    block, anywhere = pl.BlockSpec(memory_space=pltpu.VMEM), pl.BlockSpec(memory_space=pl.ANY)
    n_att = 4 * PART
    out_shape = [jax.ShapeDtypeStruct((n_att, width), F32), jax.ShapeDtypeStruct((n_att, width), BF), jax.ShapeDtypeStruct((2, width), F32), jax.ShapeDtypeStruct((3 * HEADS, HEAD), F32)]
    scratch = [pltpu.VMEM((n_att, width), BF), pltpu.SemaphoreType.DMA, pltpu.VMEM((2 * HEADS, 2 * rows, HEAD), F32), pltpu.VMEM((2 * HEADS, rows, HEAD), F32),
               pltpu.VMEM((3 * HEADS, rows, HEAD), BF), pltpu.VMEM((rows, width), BF), pltpu.SemaphoreType.DMA((2,)), pltpu.SemaphoreType.DMA((2,))]
    if with_sum:
        out_shape = [jax.ShapeDtypeStruct((rows, width), BF)] + out_shape
        scratch += [pltpu.VMEM((rows, width), BF)] + line_scratch(rows, width)
    return pl.pallas_call(
        functools.partial(att_back_kernel, n_tp, with_sum),
        out_shape=tuple(out_shape),
        in_specs=[block] * 7 + [anywhere] * 4 + [block] * 3,
        out_specs=tuple([block] * len(out_shape)),
        scratch_shapes=scratch,
        compiler_params=pltpu.CompilerParams(collective_id=3 if with_sum else 4, has_side_effects=True, vmem_limit_bytes=LIMIT),
        cost_estimate=pl.CostEstimate(flops=45_000_000_000, bytes_accessed=12_000_000, transcendentals=0),
    )(grad, hidden, gx, query, kv_all, context, lse, *options, vec, cos_tab, sin_tab)


def causal_mask(core, block, n_keys):
    row = lax.broadcasted_iota(jnp.int32, (BLOCK, n_keys), 0)
    col = lax.broadcasted_iota(jnp.int32, (BLOCK, n_keys), 1)
    part = col // BLOCK
    starts = (core, 1 - core, 3 - core, 2 + core)
    start = jnp.where(part == 0, starts[0], jnp.where(part == 1, starts[1], jnp.where(part == 2, starts[2], starts[3])))
    mine = core if block == 0 else 3 - core
    return mine * BLOCK + row >= start * BLOCK + (col - part * BLOCK)


def small_kernel(n_pp, n_tp, n_norm, rows_ref, out_ref, box, stage_sum, norm_box, send_a, recv_a, send_b, recv_b):
    stage, rank = lax.axis_index('pp'), lax.axis_index('tp')
    barrier = pltpu.get_barrier_semaphore()
    for step in range(1, n_pp):
        pl.semaphore_signal(barrier, inc=1, device_id={'pp': lax.rem(stage + step, n_pp)}, device_id_type=MESH_ID)
    for step in range(1, n_tp):
        pl.semaphore_signal(barrier, inc=1, device_id={'tp': lax.rem(rank + step, n_tp)}, device_id_type=MESH_ID)
    pl.semaphore_wait(barrier, n_pp + n_tp - 2)
    sends = []
    for step in range(1, n_pp):
        peer = lax.rem(stage + step, n_pp)
        copy = pltpu.make_async_remote_copy(
            src_ref=rows_ref.at[peer], dst_ref=box.at[step - 1], send_sem=send_a.at[step - 1],
            recv_sem=recv_a.at[step - 1], device_id={'pp': peer}, device_id_type=MESH_ID)
        copy.start()
        sends.append(copy)
    total = rows_ref[stage]
    for step, copy in enumerate(sends):
        copy.wait_recv()
        total += box[step]
    stage_sum[...] = total
    norm_box[rank] = total[:n_norm]
    shares = []
    for step in range(1, n_tp):
        copy = pltpu.make_async_remote_copy(
            src_ref=stage_sum.at[pl.ds(0, n_norm)], dst_ref=norm_box.at[rank], send_sem=send_b.at[step - 1],
            recv_sem=recv_b.at[step - 1], device_id={'tp': lax.rem(rank + step, n_tp)}, device_id_type=MESH_ID)
        copy.start()
        shares.append(copy)
    for copy in shares:
        copy.wait()
    norms = norm_box[0]
    for index in range(1, n_tp):
        norms += norm_box[index]
    out_ref[:n_norm, :] = norms
    out_ref[n_norm:, :] = total[n_norm:]
    for copy in sends:
        copy.wait_send()


def sum_small(rows, n_tp):
    n_pp, count, width = rows.shape
    n_norm = count // 2
    return pl.pallas_call(
        functools.partial(small_kernel, n_pp, n_tp, n_norm),
        out_shape=jax.ShapeDtypeStruct((count, width), F32),
        in_specs=[pl.BlockSpec(memory_space=pltpu.VMEM)],
        out_specs=pl.BlockSpec(memory_space=pltpu.VMEM),
        scratch_shapes=[pltpu.VMEM((n_pp - 1, count, width), F32), pltpu.VMEM((count, width), F32), pltpu.VMEM((n_tp, n_norm, width), F32),
                        pltpu.SemaphoreType.DMA((n_pp - 1,)), pltpu.SemaphoreType.DMA((n_pp - 1,)), pltpu.SemaphoreType.DMA((n_tp - 1,)), pltpu.SemaphoreType.DMA((n_tp - 1,))],
        compiler_params=pltpu.CompilerParams(collective_id=2, has_side_effects=True),
        cost_estimate=pl.CostEstimate(flops=8_000_000_000, bytes_accessed=200_000, transcendentals=0),
    )(rows)


def solution(mesh):
    n_stages = mesh.shape['pp']
    n_tp = mesh.shape['tp']
    swap_core = [(stage, stage ^ 1) for stage in range(n_stages)]

    def device_fn(x_in, g_out, ln1_gain, ln1_bias, w_qkv, b_qkv, w_out, b_out, ln2_gain, ln2_bias, w_up, b_up, w_down, b_down):
        stage = lax.axis_index('pp')
        core = stage % 2
        _, width = x_in.shape[2:]

        def own_tokens(array):
            blocks = lax.dynamic_index_in_dim(array, stage // 2, 0, keepdims=False).reshape(4, BLOCK, width)
            first = lax.dynamic_index_in_dim(blocks, core, 0, keepdims=False)
            second = lax.dynamic_index_in_dim(blocks, 3 - core, 0, keepdims=False)
            return jnp.concatenate([first, second], axis=0).astype(BF)

        hidden = own_tokens(x_in)
        grad = own_tokens(g_out)

        half_rot = HEAD // 8
        inv_freq = ROPE_BASE ** (-(jnp.arange(half_rot, dtype=F32) * 2.0) / (2 * half_rot))
        spot = jnp.concatenate([core * BLOCK + jnp.arange(BLOCK), (3 - core) * BLOCK + jnp.arange(BLOCK)])
        angles = spot.astype(F32)[:, None] * inv_freq[None, :]
        still = jnp.zeros((ROWS, HEAD - 2 * half_rot), F32)
        cos_tab = jnp.tile(jnp.concatenate([jnp.cos(angles), jnp.cos(angles), still + 1.0], axis=1), (1, 1))
        sin_tab = jnp.tile(jnp.concatenate([jnp.sin(angles), jnp.sin(angles), still], axis=1), (1, 1))

        wq_rows = jnp.transpose(w_qkv[0], (2, 1, 3, 0)).reshape(3 * PART, width)
        bundle = jnp.concatenate([wq_rows, w_out[0].reshape(PART, width), w_up[0], w_down[0]], axis=0)
        bias_qkv = jnp.transpose(b_qkv[0], (1, 0, 2)).reshape(3 * PART).astype(F32)
        pad = jnp.zeros((width - 3 * PART,), F32)
        vectors = jnp.stack([ln1_gain[0], ln1_bias[0], ln2_gain[0], ln2_bias[0], b_out[0].astype(F32) + b_down[0].astype(F32), b_up[0].astype(F32), jnp.concatenate([bias_qkv, pad]), jnp.zeros((width,), F32)])

        pair_a, pair_b = [(0, 2), (2, 0)], [(1, 3), (3, 1)]
        first_wave = lax.ppermute(bundle, 'pp', pair_a)
        later, first_wave = tie(bundle, first_wave)
        second_wave = lax.ppermute(later, 'pp', pair_b)
        partner = lax.ppermute(bundle, 'pp', swap_core)
        first_pass = lax.ppermute(first_wave, 'pp', [(2, 3), (0, 1)])
        all_vectors = lax.all_gather(vectors, 'pp')
        sources = {0: (bundle, partner, first_wave, first_pass), 2: (first_wave, first_pass, bundle, partner)}
        saved = []
        for layer in range(n_stages):
            vec = all_vectors[layer]
            bias_q = vec[6, :3 * PART].reshape(3 * HEADS, HEAD)
            last = layer == n_stages - 1
            result, query, kv_all, context, lse, pre_act = forward_layer(hidden, sources[layer], vec, bias_q, cos_tab, sin_tab, n_tp, not last)
            saved.append((hidden, query, kv_all, context, lse, pre_act))
            if last:
                summed = lax.psum(result, 'tp')
                break
            hidden = result
            if layer == 0:
                hidden, second_wave = tie(hidden, second_wave)
                second_pass = lax.ppermute(second_wave, 'pp', [(3, 2), (1, 0)])
                sources[1] = (partner, bundle, second_pass, second_wave)
                sources[3] = (second_pass, second_wave, partner, bundle)

        def send_near(prod_b, layer):
            return lax.ppermute(prod_b, 'pp', [(layer ^ 1, layer), (layer ^ 3, layer ^ 2)])

        def send_far(prod, layer):
            return lax.ppermute(prod, 'pp', [(layer ^ 2, layer)])

        def add_near(prod, near):
            return (prod + near.astype(F32)).astype(BF)

        small = {}
        prod, prod_b, near, far = {}, {}, {}, {}
        for layer in reversed(range(n_stages)):
            hidden, query, kv_all, context, lse, pre_act = saved[layer]
            vec = all_vectors[layer]
            key_m, key_a = (layer, 'm'), (layer, 'a')
            gx, prod[key_m], prod_b[key_m], small_m = mlp_back(grad, hidden, pre_act, sources[layer], vec)
            near[key_m] = send_near(prod_b[key_m], layer)
            above = (layer + 1, 'a')
            if above in near:
                gx, near[above] = tie(gx, near[above])
                far[above] = send_far(add_near(prod[above], near[above]), layer + 1)
            if layer < 2:
                gx, near[key_m] = tie(gx, near[key_m])
                far[key_m] = send_far(add_near(prod[key_m], near[key_m]), layer)
            out = att_back(grad, hidden, gx, query, kv_all, context, lse, sources[layer], vec, cos_tab, sin_tab, n_tp, layer > 0)
            prod[key_a], prod_b[key_a], small_a, bias_a = out[-4:]
            small[layer] = jnp.concatenate([small_a, small_m, jnp.concatenate([bias_a.reshape(1, 3 * PART), pad[None]], axis=1), jnp.zeros((1, width), F32)], axis=0)
            near[key_a] = send_near(prod_b[key_a], layer)
            if layer:
                grad = out[0]
            if layer == 3:
                grad, summed = tie(grad, summed)
            if layer > 1:
                grad, near[key_m] = tie(grad, near[key_m])
                far[key_m] = send_far(add_near(prod[key_m], near[key_m]), layer)
        far[0, 'a'] = send_far(add_near(prod[0, 'a'], near[0, 'a']), 0)

        final = (saved[-1][0].astype(F32) + all_vectors[-1][4:5] + summed.astype(F32)).astype(BF)
        gathered = lax.all_gather(final, 'pp').reshape(2, 2, 2, BLOCK, width)
        y_out = jnp.stack([gathered[:, 0, 0], gathered[:, 1, 0], gathered[:, 1, 1], gathered[:, 0, 1]], axis=1).reshape(x_in.shape)

        def total_of(key):
            return prod[key] + near[key].astype(F32) + far[key].astype(F32)

        def collect(kind):
            upper = jnp.where(stage == 3, total_of((3, kind)), total_of((2, kind)))
            (upper,) = lax.optimization_barrier((upper,))
            upper = jnp.where(stage == 1, total_of((1, kind)), upper)
            (upper,) = lax.optimization_barrier((upper,))
            return jnp.where(stage == 0, total_of((0, kind)), upper)

        small = sum_small(jnp.stack([small[layer] for layer in range(n_stages)]), n_tp)
        norms = small
        grad_att, grad_mlp = collect('a'), collect('m')
        grad_qkv = jnp.transpose(grad_att[:3 * PART].reshape(3, HEADS, HEAD, width), (3, 1, 0, 2))
        grads = (
            norms[0], norms[1], grad_qkv, jnp.transpose(small[6, :3 * PART].reshape(3, HEADS, HEAD), (1, 0, 2)),
            grad_att[3 * PART:].reshape(HEADS, HEAD, width), small[4], norms[2], norms[3],
            grad_mlp[:width], small[5], grad_mlp[width:], small[4])
        return tuple([y_out] + [item[None] for item in grads])

    return jax.shard_map(device_fn, mesh=mesh, in_specs=(P('dp'), P('dp')) + STAGE_SPECS, out_specs=(P('dp'),) + GRAD_SPECS, check_vma=False)
```

time: 790 us -> 620 us (0.78)
  matrix products: 147 us -> 0 us
  Pallas kernels: 262 us -> 383 us
  other arithmetic: 112 us -> 69.1 us
  local copies, waits for them, and re-layouts: 62.4 us -> 34.1 us
  blocking collectives: 31 us -> 5.58 us
  waiting for transfers between devices: 79.8 us -> 56.8 us
  starting transfers between devices: 64.2 us -> 46.1 us
    dot_general x200 -> x0, matrix products: 147 us -> none  [dot(): lax.dot_general(left, right, (((left_dim,), (right_dim,)), ((), ())), pre...]
    pallas_call x7 -> x13, Pallas kernels: 262 us -> 383 us  [the longest x4 168 us: att_back(): pl.pallas_call(functools.partial(att_back_kernel, n_tp, with_sum), out_sh...]
    psum x1 -> x0, blocking collectives: 25.5 us -> none  [device_fn(): norms = lax.psum(small[:4], 'tp')]
    ppermute x18, waiting for transfers between devices: 79.8 us -> 55.3 us  [the longest x1 39.5 us: device_fn(): first_wave = lax.ppermute(bundle, 'pp', pair_a)]
    reduce_sum x24 -> x0, other arithmetic: 20.9 us -> none  [the longest x4 5.45 us: normalise(): center = hidden_f - jnp.mean(hidden_f, axis=-1, keepdims=True)]
    unnamed x838 -> x47, local copies, waits for them, and re-layouts: 22.3 us -> 3.4 us
    ppermute x18, starting transfers between devices: 59.5 us -> 41.4 us  [the longest x8 17.2 us: send_far(): return lax.ppermute(prod, 'pp', [(layer ^ 2, layer)])]
    convert_element_type x29 -> x9, other arithmetic: 40.9 us -> 29 us  [the longest x8 26.5 us: add_near(): return (prod + near.astype(F32)).astype(BF)]
  transfers between devices with their start and end apart: 23 -> 23, of which waited for: 3 -> 4; matrix products, arithmetic and copies ran while one was open for 23% -> 15% of each run, Pallas kernels for 18% -> 47%
where the time goes in v2:
time: 620 us; the launch traced here: 610 us
  Pallas kernels  383 us (62%)
  other arithmetic  69.1 us (11%)
  waiting for transfers between devices  56.8 us (9%)
  starting transfers between devices  46.1 us (7%)
  local copies, waits for them, and re-layouts  34.1 us (6%)
  between operations  15 us (2%)
    pallas_call x4, Pallas kernels, att_back(): pl.pallas_call(functools.partial(att_back_kernel, n_tp, with_sum), out_sh...  168 us
    pallas_call x4, Pallas kernels, forward_layer(): pl.pallas_call(functools.partial(forward_kernel, n_tp, with_sum), out_sha...  143 us
    pallas_call x4, Pallas kernels, mlp_back(): pl.pallas_call(mlp_back_kernel, out_shape=(jax.ShapeDtypeStruct((rows, wi...  40.1 us
    ppermute x1, waiting for transfers between devices, device_fn(): first_wave = lax.ppermute(bundle, 'pp', pair_a)  39.5 us
    pallas_call x1, Pallas kernels, sum_small(): pl.pallas_call(functools.partial(small_kernel, n_pp, n_tp, n_norm), out_s...  32 us
    convert_element_type x8, other arithmetic, add_near(): return (prod + near.astype(F32)).astype(BF)  26.5 us
    ppermute x8, starting transfers between devices, send_far(): return lax.ppermute(prod, 'pp', [(layer ^ 2, layer)])  17.2 us
    ppermute x8, starting transfers between devices, send_near(): lax.ppermute(prod_b, 'pp', [(layer ^ 1, layer), (layer ^ 3, layer ^ 2)])  16.8 us
  transfers between devices with their start and end apart: 23, of which 4 were waited for; matrix products, arithmetic and copies ran while one was open for 15% of the time, Pallas kernels for 47%

profile of v2, /device:TPU:0, one launch (start us, length us, event | category | flops | bytes accessed | tf_op | source)
XLA Modules:
  0.0 609.5 jit_solution(12852852290529531483)
XLA Ops:
  7.2 1.3 copy.42
  8.8 1.5 pad_maximum_fusion.opt0.opt1.opt2.opt3
  10.3 4.9 collective-permute-start.1
  15.3 39.5 %collective-permute-done.1.opt2.opt0 = bf16[2304,768]{1,0:T(8,128)(2,1)} collective-permute-done((bf16[2304,768]{1,0:T(8,128)(2,1)S(1)}, bf16[2304,768]{1,0:T(8,128)(2,1)}, u32[]{:S(2)}, u32[]{:S(2)}) %collective-permute-start.1) | collective-permute-done | bytes 3538976 | tf_op jit(solution)/shard_map/ppermute | solution.py:509
  54.8 3.1 collective-permute-start.2
  59.9 1.4 stack.31
  61.3 5.6 all-gather
  68.2 1.4 reshape_squeeze.19.bq_ref
  69.5 3.8 constant_dynamic-slice_fusion
  77.6 2.4 collective-permute-start.3
  80.1 43.7 %shard_map.237 = (bf16[512,768]{1,0:T(8,128)(2,1)}, bf16[3,512,64]{2,1,0:T(8,128)(2,1)}, bf16[6,1024,64]{2,1,0:T(8,128)(2,1)}, bf16[3,512,64]{2,1,0:T(8,128)(2,1...) custom-call(bf16[512,768]{1,0:T(8,128)(2,1)} %pad_maximum_fusion.2.h_ref, bf16[2304,768]{1,0:T(8,128)(2,1)} %copy-done.7, ...), custom_call_target="tpu_custom_call" | custom-call | flops 40000000000 | bytes 8000000 | tf_op jit(solution)/shard_map/pallas_call | solution.py:231
  123.8 1.5 collective-permute-start.4
  127.3 1.3 slice_reduce_fusion
  130.7 1.4 collective-permute-done.4.opt2.opt0
  132.1 1.8 copy-done.22
  133.9 41.6 %shard_map.238 = (bf16[512,768]{1,0:T(8,128)(2,1)}, bf16[3,512,64]{2,1,0:T(8,128)(2,1)}, bf16[6,1024,64]{2,1,0:T(8,128)(2,1)}, bf16[3,512,64]{2,1,0:T(8,128)(2,1...) custom-call(bf16[512,768]{1,0:T(8,128)(2,1)} %get-tuple-element.95.h_ref, ...), custom_call_target="tpu_custom_call" | custom-call | flops 40000000000 | bytes 8000000 | tf_op jit(solution)/shard_map/pallas_call | solution.py:231
  175.6 41.3 %shard_map.239 = (bf16[512,768]{1,0:T(8,128)(2,1)}, bf16[3,512,64]{2,1,0:T(8,128)(2,1)}, bf16[6,1024,64]{2,1,0:T(8,128)(2,1)}, bf16[3,512,64]{2,1,0:T(8,128)(2,1...) custom-call(bf16[512,768]{1,0:T(8,128)(2,1)} %get-tuple-element.97.h_ref, ...), custom_call_target="tpu_custom_call" | custom-call | flops 40000000000 | bytes 8000000 | tf_op jit(solution)/shard_map/pallas_call | solution.py:231
  216.9 16.3 %shard_map.240 = (bf16[512,768]{1,0:T(8,128)(2,1)}, bf16[3,512,64]{2,1,0:T(8,128)(2,1)}, bf16[6,1024,64]{2,1,0:T(8,128)(2,1)}, bf16[3,512,64]{2,1,0:T(8,128)(2,1...) custom-call(bf16[512,768]{1,0:T(8,128)(2,1)} %get-tuple-element.98.h_ref, bf16[2304,768]{1,0:T(8,128)(2,1)} %copy-done.22, ...), custom_call_target="tpu_custom_call" | custom-call | flops 40000000000 | bytes 8000000 | tf_op jit(solution)/shard_map/pallas_call | solution.py:231
  233.3 9.9 %shard_map.241 = (f32[512,768]{1,0:T(8,128)}, f32[1536,768]{1,0:T(8,128)}, bf16[1536,768]{1,0:T(8,128)(2,1)}, f32[4,768]{1,0:T(4,128)}) custom-call(bf16[512,768]{1,0:T(8,128)(2,1)} %pad_maximum_fusion.3.g_ref, bf16[512,768]{1,0:T(8,128)(2,1)} %get-tuple-element.98.h_ref, f32[512,768]{1,0:T(8,128)} %get-tuple-element.99.pre_ref, ...), custom_call_target="tpu_custom_call" | custom-call | flops 10000000000 | bytes 12000000 | tf_op jit(solution)/shard_map/pallas_call | solution.py:279
  243.2 2.9 collective-permute-start.5
  246.1 56.9 %shard_map.242 = (bf16[512,768]{1,0:T(8,128)(2,1)}, f32[768,768]{1,0:T(8,128)}, bf16[768,768]{1,0:T(8,128)(2,1)}, f32[2,768]{1,0:T(2,128)}, f32[9,64]{1,0:T(8,128)}) custom-call(bf16[512,768]{1,0:T(8,128)(2,1)} %pad_maximum_fusion.3.g_ref, bf16[512,768]{1,0:T(8,128)(2,1)} %get-tuple-element.98.h_ref, f32[512,768]{1,0:T(8,128)} %get-tuple-element.100.gx_ref, ...), custom_call_target="tpu_custom_call" | custom-call | flops 44999999488 | bytes 12000000 | tf_op jit(solution)/shard_map/pallas_call | solution.py:399
  303.1 1.4 reshape.93
  304.4 1.5 collective-permute-start.6
  306.0 2.5 add_convert_fusion
  308.5 4.3 fusion.2
  312.8 2.2 collective-permute-start.19
  315.0 10.4 %shard_map.243 = (f32[512,768]{1,0:T(8,128)}, f32[1536,768]{1,0:T(8,128)}, bf16[1536,768]{1,0:T(8,128)(2,1)}, f32[4,768]{1,0:T(4,128)}) custom-call(bf16[512,768]{1,0:T(8,128)(2,1)} %get-tuple-element.110.g_ref, bf16[512,768]{1,0:T(8,128)(2,1)} %get-tuple-element.97.h_ref, f32[512,768]{1,0:T(8,128)} %get-tuple-element.111.pre_ref, ...), custom_call_target="tpu_custom_call" | custom-call | flops 10000000000 | bytes 12000000 | tf_op jit(solution)/shard_map/pallas_call | solution.py:279
  325.4 1.3 collective-permute-start.7
  326.7 46.1 %shard_map.244 = (bf16[512,768]{1,0:T(8,128)(2,1)}, f32[768,768]{1,0:T(8,128)}, bf16[768,768]{1,0:T(8,128)(2,1)}, f32[2,768]{1,0:T(2,128)}, f32[9,64]{1,0:T(8,128)}) custom-call(bf16[512,768]{1,0:T(8,128)(2,1)} %get-tuple-element.110.g_ref, bf16[512,768]{1,0:T(8,128)(2,1)} %get-tuple-element.97.h_ref, f32[512,768]{1,0:T(8,128)} %get-tuple-element.114.gx_ref, ...), custom_call_target="tpu_custom_call" | custom-call | flops 44999999488 | bytes 12000000 | tf_op jit(solution)/shard_map/pallas_call | solution.py:399
  372.8 1.3 collective-permute-start.8
  374.1 9.9 %shard_map.245 = (f32[512,768]{1,0:T(8,128)}, f32[1536,768]{1,0:T(8,128)}, bf16[1536,768]{1,0:T(8,128)(2,1)}, f32[4,768]{1,0:T(4,128)}) custom-call(bf16[512,768]{1,0:T(8,128)(2,1)} %get-tuple-element.121.g_ref, bf16[512,768]{1,0:T(8,128)(2,1)} %get-tuple-element.95.h_ref, f32[512,768]{1,0:T(8,128)} %get-tuple-element.122.pre_ref, ...), custom_call_target="tpu_custom_call" | custom-call | flops 10000000000 | bytes 12000000 | tf_op jit(solution)/shard_map/pallas_call | solution.py:279
  384.0 5.5 collective-permute-start.9
  389.5 2.9 fusion.6
  393.1 1.7 collective-permute-start.15
  394.8 3.4 fusion.7
  398.2 4.2 collective-permute-start.16
  402.4 3.9 fusion.3
  406.3 2.7 collective-permute-start.20
  408.9 2.0 slice_bitcast_fusion.5
  411.5 1.9 copy.48
  413.3 6.6 %collective-permute-done.16 = bf16[768,768]{1,0:T(8,128)(2,1)} collective-permute-done((bf16[768,768]{1,0:T(8,128)(2,1)}, bf16[768,768]{1,0:T(8,128)(2,1)}, u32[]{:S(2)}, u32[]{:S(2)}) %collective-permute-start.16) | collective-permute-done | bytes 1179680 | tf_op jit(solution)/shard_map/ppermute | solution.py:537
  419.9 4.3 add_select_fusion.3
  424.2 43.8 %shard_map.246 = (bf16[512,768]{1,0:T(8,128)(2,1)}, f32[768,768]{1,0:T(8,128)}, bf16[768,768]{1,0:T(8,128)(2,1)}, f32[2,768]{1,0:T(2,128)}, f32[9,64]{1,0:T(8,128)}) custom-call(bf16[512,768]{1,0:T(8,128)(2,1)} %get-tuple-element.121.g_ref, bf16[512,768]{1,0:T(8,128)(2,1)} %get-tuple-element.95.h_ref, f32[512,768]{1,0:T(8,128)} %get-tuple-element.127.gx_ref, ...), custom_call_target="tpu_custom_call" | custom-call | flops 44999999488 | bytes 12000000 | tf_op jit(solution)/shard_map/pallas_call | solution.py:399
  468.0 1.7 collective-permute-start.10
  469.8 9.9 %shard_map.247 = (f32[512,768]{1,0:T(8,128)}, f32[1536,768]{1,0:T(8,128)}, bf16[1536,768]{1,0:T(8,128)(2,1)}, f32[4,768]{1,0:T(4,128)}) custom-call(bf16[512,768]{1,0:T(8,128)(2,1)} %get-tuple-element.132.g_ref, bf16[512,768]{1,0:T(8,128)(2,1)} %pad_maximum_fusion.2.h_ref, f32[512,768]{1,0:T(8,128)} %get-tuple-element.133.pre_ref, ...), custom_call_target="tpu_custom_call" | custom-call | flops 10000000000 | bytes 12000000 | tf_op jit(solution)/shard_map/pallas_call | solution.py:279
  479.7 1.3 collective-permute-start.11
  481.0 9.4 %add_select_fusion = f32[1536,768]{1,0:T(8,128)} fusion(bf16[1536,768]{1,0:T(8,128)(2,1)} %collective-permute-done.20, bf16[1536,768]{1,0:T(8,128)(2,1)} %collective-permute-done.19, f32[1536,768]{1,0:T(8,128)} %get-tuple-element.167, bf16[1536,768]{1,0:T(8,128)(2,1)S(1)} %collective-permute-done.5, f32[1536,768]{1,0:T(8,128)} %get-tuple-element.169, ...), kind=kLoop, calls=%fused_computation | loop fusion | flops 10616832 | bytes 23592960 | tf_op jit(solution)/shard_map/jit(_where)/select_n | solution.py:578
  491.0 5.2 fusion.1
  496.2 2.0 collective-permute-start.18
  499.5 1.8 collective-permute-start.14
  501.3 3.8 fusion
  506.4 21.0 %shard_map.248 = (f32[768,768]{1,0:T(8,128)}, bf16[768,768]{1,0:T(8,128)(2,1)}, f32[2,768]{1,0:T(2,128)}, f32[9,64]{1,0:T(8,128)}) custom-call(bf16[512,768]{1,0:T(8,128)(2,1)} %get-tuple-element.132.g_ref, bf16[512,768]{1,0:T(8,128)(2,1)} %pad_maximum_fusion.2.h_ref, f32[512,768]{1,0:T(8,128)} %get-tuple-element.138.gx_ref, ...), custom_call_target="tpu_custom_call" | custom-call | flops 44999999488 | bytes 12000000 | tf_op jit(solution)/shard_map/pallas_call | solution.py:399
  527.5 8.1 %add_select_fusion.1 = f32[1536,768]{1,0:T(8,128)} fusion(f32[1536,768]{1,0:T(8,128)} %add_select_fusion, bf16[1536,768]{1,0:T(8,128)(2,1)} %collective-permute-done.18, f32[1536,768]{1,0:T(8,128)} %get-tuple-element.165, bf16[1536,768]{1,0:T(8,128)(2,1)} %collective-permute-done.9, pred[]{:T(512)S(6)} %eq.15), kind=kLoop, calls=%fused_computation.3 | loop fusion | flops 5898240 | bytes 18874368 | tf_op jit(solution)/shard_map/jit(_where)/select_n | solution.py:580
  535.6 1.3 reshape.90
  539.8 32.0 %shard_map.249 = f32[8,768]{1,0:T(8,128)} custom-call(f32[4,8,768]{2,1,0:T(8,128)} %pad_maximum_fusion.4.rows_ref), custom_call_target="tpu_custom_call" | custom-call | flops 8000000000 | bytes 200000 | tf_op jit(solution)/shard_map/pallas_call | solution.py:463
  573.3 1.7 fusion.16
  574.9 2.6 add_select_fusion.4
  577.7 1.8 fusion.4
  579.5 1.3 collective-permute-start.13
  580.8 5.1 add_select_fusion.2
  585.8 2.5 slice_bitcast_fusion
  588.3 9.2 %collective-permute-done.13 = bf16[768,768]{1,0:T(8,128)(2,1)S(1)} collective-permute-done((bf16[768,768]{1,0:T(8,128)(2,1)S(1)}, bf16[768,768]{1,0:T(8,128)(2,1)S(1)}, u32[]{:S(2)}, u32[]{:S(2)}) %collective-permute-start.13) | collective-permute-done | bytes 1179680 | tf_op jit(solution)/shard_map/ppermute | solution.py:537
  597.5 1.9 add_select_fusion.5
  600.4 1.3 copy.56
  (109 shorter events, 22.4 us)
Async XLA Ops:
  7.2 298.8 %all-reduce.7.cloned.1.call-start = ((), (), s32[]{:S(2)}) async-start(), calls=%async_computation | async-start | bytes 1572864 | tf_op jit(solution)/shard_map/psum | solution.py:524
  7.2 1.5 copy-start.8
  8.8 50.3 %copy-start.19 = (bf16[1,3,3,64]{3,2,1,0:T(4,128)(2,1)S(1)}, bf16[1,3,3,64]{3,2,1,0:T(4,128)(2,1)}, u32[]{:S(2)}) copy-start(bf16[1,3,3,64]{3,2,1,0:T(4,128)(2,1)} %param.19) | copy-start | bytes 3460
  8.8 51.1 %copy-start.18 = (f32[1,768]{1,0:T(1,128)S(1)}, f32[1,768]{1,0:T(1,128)}, u32[]{:S(2)}) copy-start(f32[1,768]{1,0:T(1,128)} %param.16) | copy-start | bytes 9220
  10.3 67.3 %copy-start.7 = (bf16[2304,768]{1,0:T(8,128)(2,1)}, bf16[2304,768]{1,0:T(8,128)(2,1)S(1)}, u32[]{:S(2)}) copy-start(bf16[2304,768]{1,0:T(8,128)(2,1)S(1)} %pad_maximum_fusion.opt0.opt1.opt2.opt3) | copy-start | bytes 10616836
  10.3 44.5 %collective-permute-start.1 = (bf16[2304,768]{1,0:T(8,128)(2,1)S(1)}, bf16[2304,768]{1,0:T(8,128)(2,1)}, u32[]{:S(2)}, u32[]{:S(2)}) collective-permute-start(bf16[2304,768]{1,0:T(8,128)(2,1)S(1)} %pad_maximum_fusion.opt0.opt1.opt2.opt3), channel_id=1, source_target_pairs={{0,2},{2,0},{4,6},{6,4},{8,10},{10,8},{12,14},{14,12},{16,18},{18,... | collective-permute-start | bytes 10616840 | tf_op jit(solution)/shard_map/ppermute | solution.py:509
  15.2 64.9 %collective-permute-start = (bf16[2304,768]{1,0:T(8,128)(2,1)S(1)}, bf16[2304,768]{1,0:T(8,128)(2,1)}, u32[]{:S(2)}, u32[]{:S(2)}) collective-permute-start(bf16[2304,768]{1,0:T(8,128)(2,1)S(1)} %pad_maximum_fusion.opt0.opt1.opt2.opt3), channel_id=1, source_target_pairs={{0,1},{1,0},{2,3},{3,2},{4,5},{5,4},{6,7},{7,6},{8,9},{9,8},{10,11... | collective-permute-start | bytes 10616840 | tf_op jit(solution)/shard_map/ppermute | solution.py:512
  54.8 25.3 %collective-permute-start.2 = (bf16[2304,768]{1,0:T(8,128)(2,1)}, bf16[2304,768]{1,0:T(8,128)(2,1)}, u32[]{:S(2)}, u32[]{:S(2)}) collective-permute-start(bf16[2304,768]{1,0:T(8,128)(2,1)} %collective-permute-done.1.opt2.opt0), channel_id=1, source_target_pairs={{2,3},{0,1},{6,7},{4,5},{10,11},{8,9},{14,15},{12,13},{18,19},{16,... | collective-permute-start | bytes 10616840 | tf_op jit(solution)/shard_map/ppermute | solution.py:513
  59.9 63.9 %copy-start.11 = (f32[1,768]{1,0:T(1,128)}, f32[1,768]{1,0:T(1,128)S(1)}, u32[]{:S(2)}) copy-start(f32[1,768]{1,0:T(1,128)S(1)} %broadcast.42) | copy-start | bytes 9220
  66.9 0.6 copy-start.9
  73.3 1.0 copy-start.10
  73.3 2.6 copy-start.20
  73.3 3.5 copy-start.21
  77.6 46.2 %collective-permute-start.3 = (bf16[2304,768]{1,0:T(8,128)(2,1)S(1)}, bf16[2304,768]{1,0:T(8,128)(2,1)}, u32[]{:S(2)}, u32[]{:S(2)}) collective-permute-start(bf16[2304,768]{1,0:T(8,128)(2,1)S(1)} %pad_maximum_fusion.opt0.opt1.opt2.opt3), channel_id=1, source_target_pairs={{1,3},{3,1},{5,7},{7,5},{9,11},{11,9},{13,15},{15,13},{17,19},{19,... | collective-permute-start | bytes 10616840 | tf_op jit(solution)/shard_map/ppermute | solution.py:511
  123.8 8.3 %collective-permute-start.4 = (bf16[2304,768]{1,0:T(8,128)(2,1)}, bf16[2304,768]{1,0:T(8,128)(2,1)S(1)}, u32[]{:S(2)}, u32[]{:S(2)}) collective-permute-start(bf16[2304,768]{1,0:T(8,128)(2,1)} %collective-permute-done.3.opt3.opt1), channel_id=1, source_target_pairs={{3,2},{1,0},{7,6},{5,4},{11,10},{9,8},{15,14},{13,12},{19,18},{17,... | collective-permute-start | bytes 10616840 | tf_op jit(solution)/shard_map/ppermute | solution.py:529
  132.1 1.8 copy-start.22
  233.2 175.7 %all-gather.4.cloned.1.call-start = ((), (), s32[]{:S(2)}) async-start(), calls=%async_computation.1 | async-start | bytes 3932160 | tf_op jit(solution)/shard_map/all_gather | solution.py:571
  243.2 65.3 %collective-permute-start.5 = (bf16[1536,768]{1,0:T(8,128)(2,1)}, bf16[1536,768]{1,0:T(8,128)(2,1)S(1)}, u32[]{:S(2)}, u32[]{:S(2)}) collective-permute-start(bf16[1536,768]{1,0:T(8,128)(2,1)} %get-tuple-element.109), channel_id=1, source_target_pairs={{2,3},{0,1},{6,7},{4,5},{10,11},{8,9},{14,15},{12,13},{18,19},{16,... | collective-permute-start | bytes 7077896 | tf_op jit(solution)/shard_map/ppermute | solution.py:534
  246.1 59.9 %copy-start.13 = (f32[768]{0:T(1024)S(1)}, f32[768]{0:T(1024)}, u32[]{:S(2)}) copy-start(f32[768]{0:T(1024)} %slice_reduce_fusion) | copy-start | bytes 9220
  304.4 21.0 %collective-permute-start.6 = (bf16[768,768]{1,0:T(8,128)(2,1)}, bf16[768,768]{1,0:T(8,128)(2,1)S(1)}, u32[]{:S(2)}, u32[]{:S(2)}) collective-permute-start(bf16[768,768]{1,0:T(8,128)(2,1)} %get-tuple-element.113), channel_id=1, source_target_pairs={{2,3},{0,1},{6,7},{4,5},{10,11},{8,9},{14,15},{12,13},{18,19},{16,... | collective-permute-start | bytes 3538952 | tf_op jit(solution)/shard_map/ppermute | solution.py:534
  312.8 168.2 %collective-permute-start.19 = (bf16[1536,768]{1,0:T(8,128)(2,1)}, bf16[1536,768]{1,0:T(8,128)(2,1)}, u32[]{:S(2)}, u32[]{:S(2)}) collective-permute-start(bf16[1536,768]{1,0:T(8,128)(2,1)} %fusion.2), channel_id=1, source_target_pairs={{1,3},{5,7},{9,11},{13,15},{17,19},{21,23},{25,27},{29,31}} | collective-permute-start | bytes 7077896 | tf_op jit(solution)/shard_map/ppermute | solution.py:537
  325.4 48.7 %collective-permute-start.7 = (bf16[1536,768]{1,0:T(8,128)(2,1)}, bf16[1536,768]{1,0:T(8,128)(2,1)}, u32[]{:S(2)}, u32[]{:S(2)}) collective-permute-start(bf16[1536,768]{1,0:T(8,128)(2,1)} %get-tuple-element.120), channel_id=1, source_target_pairs={{3,2},{1,0},{7,6},{5,4},{11,10},{9,8},{15,14},{13,12},{19,18},{17,... | collective-permute-start | bytes 7077896 | tf_op jit(solution)/shard_map/ppermute | solution.py:534
  372.8 22.0 %collective-permute-start.8 = (bf16[768,768]{1,0:T(8,128)(2,1)}, bf16[768,768]{1,0:T(8,128)(2,1)}, u32[]{:S(2)}, u32[]{:S(2)}) collective-permute-start(bf16[768,768]{1,0:T(8,128)(2,1)} %get-tuple-element.124), channel_id=1, source_target_pairs={{3,2},{1,0},{7,6},{5,4},{11,10},{9,8},{15,14},{13,12},{19,18},{17,... | collective-permute-start | bytes 3538952 | tf_op jit(solution)/shard_map/ppermute | solution.py:534
  384.0 40.2 %collective-permute-start.9 = (bf16[1536,768]{1,0:T(8,128)(2,1)}, bf16[1536,768]{1,0:T(8,128)(2,1)}, u32[]{:S(2)}, u32[]{:S(2)}) collective-permute-start(bf16[1536,768]{1,0:T(8,128)(2,1)} %get-tuple-element.126), channel_id=1, source_target_pairs={{0,1},{2,3},{4,5},{6,7},{8,9},{10,11},{12,13},{14,15},{16,17},{18,... | collective-permute-start | bytes 7077896 | tf_op jit(solution)/shard_map/ppermute | solution.py:534
  389.5 2.9 copy-start.17
  393.1 20.3 %collective-permute-start.15 = (bf16[768,768]{1,0:T(8,128)(2,1)}, bf16[768,768]{1,0:T(8,128)(2,1)}, u32[]{:S(2)}, u32[]{:S(2)}) collective-permute-start(bf16[768,768]{1,0:T(8,128)(2,1)} %fusion.6), channel_id=1, source_target_pairs={{1,3},{5,7},{9,11},{13,15},{17,19},{21,23},{25,27},{29,31}} | collective-permute-start | bytes 3538952 | tf_op jit(solution)/shard_map/ppermute | solution.py:537
  394.8 7.6 %copy-start = (f32[1536,768]{1,0:T(8,128)S(1)}, f32[1536,768]{1,0:T(8,128)}, u32[]{:S(2)}) copy-start(f32[1536,768]{1,0:T(8,128)} %get-tuple-element.169) | copy-start | bytes 14155780
  398.2 21.8 %collective-permute-start.16 = (bf16[768,768]{1,0:T(8,128)(2,1)}, bf16[768,768]{1,0:T(8,128)(2,1)}, u32[]{:S(2)}, u32[]{:S(2)}) collective-permute-start(bf16[768,768]{1,0:T(8,128)(2,1)} %fusion.7), channel_id=1, source_target_pairs={{0,2},{4,6},{8,10},{12,14},{16,18},{20,22},{24,26},{28,30}} | collective-permute-start | bytes 3538952 | tf_op jit(solution)/shard_map/ppermute | solution.py:537
  406.3 74.7 %collective-permute-start.20 = (bf16[1536,768]{1,0:T(8,128)(2,1)}, bf16[1536,768]{1,0:T(8,128)(2,1)}, u32[]{:S(2)}, u32[]{:S(2)}) collective-permute-start(bf16[1536,768]{1,0:T(8,128)(2,1)} %fusion.3), channel_id=1, source_target_pairs={{0,2},{4,6},{8,10},{12,14},{16,18},{20,22},{24,26},{28,30}} | collective-permute-start | bytes 7077896 | tf_op jit(solution)/shard_map/ppermute | solution.py:537
  411.4 8.5 %copy-start.4 = (f32[768,768]{1,0:T(8,128)S(1)}, f32[768,768]{1,0:T(8,128)}, u32[]{:S(2)}) copy-start(f32[768,768]{1,0:T(8,128)} %get-tuple-element.159) | copy-start | bytes 7077892
  411.4 8.5 %copy-start.6 = (f32[768,768]{1,0:T(8,128)S(1)}, f32[768,768]{1,0:T(8,128)}, u32[]{:S(2)}) copy-start(f32[768,768]{1,0:T(8,128)} %get-tuple-element.161) | copy-start | bytes 7077892
  468.0 30.2 %collective-permute-start.10 = (bf16[768,768]{1,0:T(8,128)(2,1)}, bf16[768,768]{1,0:T(8,128)(2,1)S(1)}, u32[]{:S(2)}, u32[]{:S(2)}) collective-permute-start(bf16[768,768]{1,0:T(8,128)(2,1)} %get-tuple-element.135), channel_id=1, source_target_pairs={{0,1},{2,3},{4,5},{6,7},{8,9},{10,11},{12,13},{14,15},{16,17},{18,... | collective-permute-start | bytes 3538952 | tf_op jit(solution)/shard_map/ppermute | solution.py:534
  479.7 10.7 %copy-start.16 = (f32[9,64]{1,0:T(8,128)S(1)}, f32[9,64]{1,0:T(8,128)}, u32[]{:S(2)}) copy-start(f32[9,64]{1,0:T(8,128)} %get-tuple-element.148) | copy-start | bytes 6916
  479.7 21.6 %collective-permute-start.11 = (bf16[1536,768]{1,0:T(8,128)(2,1)}, bf16[1536,768]{1,0:T(8,128)(2,1)}, u32[]{:S(2)}, u32[]{:S(2)}) collective-permute-start(bf16[1536,768]{1,0:T(8,128)(2,1)} %get-tuple-element.137), channel_id=1, source_target_pairs={{1,0},{3,2},{5,4},{7,6},{9,8},{11,10},{13,12},{15,14},{17,16},{19,... | collective-permute-start | bytes 7077896 | tf_op jit(solution)/shard_map/ppermute | solution.py:534
  491.0 7.2 %copy-start.3 = (f32[768,768]{1,0:T(8,128)S(1)}, f32[768,768]{1,0:T(8,128)}, u32[]{:S(2)}) copy-start(f32[768,768]{1,0:T(8,128)} %get-tuple-element.157) | copy-start | bytes 7077892
  496.2 31.3 %collective-permute-start.18 = (bf16[1536,768]{1,0:T(8,128)(2,1)}, bf16[1536,768]{1,0:T(8,128)(2,1)}, u32[]{:S(2)}, u32[]{:S(2)}) collective-permute-start(bf16[1536,768]{1,0:T(8,128)(2,1)} %fusion.1), channel_id=1, source_target_pairs={{3,1},{7,5},{11,9},{15,13},{19,17},{23,21},{27,25},{31,29}} | collective-permute-start | bytes 7077896 | tf_op jit(solution)/shard_map/ppermute | solution.py:537
  498.2 3.1 copy-start.1
  499.5 75.5 %collective-permute-start.14 = (bf16[768,768]{1,0:T(8,128)(2,1)}, bf16[768,768]{1,0:T(8,128)(2,1)}, u32[]{:S(2)}, u32[]{:S(2)}) collective-permute-start(bf16[768,768]{1,0:T(8,128)(2,1)} %fusion.5), channel_id=1, source_target_pairs={{3,1},{7,5},{11,9},{15,13},{19,17},{23,21},{27,25},{31,29}} | collective-permute-start | bytes 3538952 | tf_op jit(solution)/shard_map/ppermute | solution.py:537
  505.1 75.6 %collective-permute-start.17 = (bf16[1536,768]{1,0:T(8,128)(2,1)}, bf16[1536,768]{1,0:T(8,128)(2,1)}, u32[]{:S(2)}, u32[]{:S(2)}) collective-permute-start(bf16[1536,768]{1,0:T(8,128)(2,1)} %fusion), channel_id=1, source_target_pairs={{2,0},{6,4},{10,8},{14,12},{18,16},{22,20},{26,24},{30,28}} | collective-permute-start | bytes 7077896 | tf_op jit(solution)/shard_map/ppermute | solution.py:537
  527.5 10.8 %copy-start.12 = (f32[1,768]{1,0:T(1,128)S(1)}, f32[1,768]{1,0:T(1,128)}, u32[]{:S(2)}) copy-start(f32[1,768]{1,0:T(1,128)} %copy-done.11) | copy-start | bytes 9220
  527.5 10.8 %copy-start.14 = (f32[4,768]{1,0:T(4,128)S(1)}, f32[4,768]{1,0:T(4,128)}, u32[]{:S(2)}) copy-start(f32[4,768]{1,0:T(4,128)} %get-tuple-element.153) | copy-start | bytes 36868
  537.0 40.6 %collective-permute-start.12 = (bf16[768,768]{1,0:T(8,128)(2,1)}, bf16[768,768]{1,0:T(8,128)(2,1)}, u32[]{:S(2)}, u32[]{:S(2)}) collective-permute-start(bf16[768,768]{1,0:T(8,128)(2,1)} %get-tuple-element.156), channel_id=1, source_target_pairs={{1,0},{3,2},{5,4},{7,6},{9,8},{11,10},{13,12},{15,14},{17,16},{19,... | collective-permute-start | bytes 3538952 | tf_op jit(solution)/shard_map/ppermute | solution.py:534
  574.9 26.8 %copy-start.15 = (f32[1,768]{1,0:T(1,128)}, f32[1,768]{1,0:T(1,128)S(1)}, u32[]{:S(2)}) copy-start(f32[1,768]{1,0:T(1,128)S(1)} %get-tuple-element.230) | copy-start | bytes 9220
  574.9 2.7 copy-start.5
  577.7 3.1 copy-start.2
  579.5 18.1 %collective-permute-start.13 = (bf16[768,768]{1,0:T(8,128)(2,1)S(1)}, bf16[768,768]{1,0:T(8,128)(2,1)S(1)}, u32[]{:S(2)}, u32[]{:S(2)}) collective-permute-start(bf16[768,768]{1,0:T(8,128)(2,1)S(1)} %fusion.4), channel_id=1, source_target_pairs={{2,0},{6,4},{10,8},{14,12},{18,16},{22,20},{26,24},{30,28}} | collective-permute-start | bytes 3538952 | tf_op jit(solution)/shard_map/ppermute | solution.py:537
Sparse Core Ops, SparseCore 0:
  233.4 52.3 all-reduce.6
  308.6 32.2 all-gather.3
